TPU v7x, 32 devices: a whole 2x2x4 slice. The times are simulated.
32 devices in a mesh: parts: 1, seq: 8 (over z, y), head: 2 (over x), rep: 2 (over core).
Axes of the slice: x: 2, y: 2, z: 4, core: 2. Of those that a mesh axis runs over, the one named last changes fastest.
Arguments:
- residual: bfloat16 [16, 8192], P(('parts', 'head'), ('seq', 'rep')), may hold values from -48 to 48
- coefficients: float32 [16, 16], P(('parts', 'head')), may hold values from -6 to 6
- directions: float32 [16, 8192], P(None, ('seq', 'rep')), may hold values from -1.5 to 1.5
- attn_gain: float32 [8192], P(('seq', 'rep')), may hold values from 0.25 to 1.75
- mlp_gain: float32 [8192], replicated, may hold values from 0.25 to 1.75
- w_query: bfloat16 [8192, 8192], P(('seq', 'rep'), 'head'), may hold values from -0.0625 to 0.0625
- w_output: bfloat16 [8192, 8192], P('head', ('seq', 'rep')), may hold values from -0.0625 to 0.0625
- w_gate: bfloat16 [8192, 14336], P('head', ('seq', 'rep')), may hold values from -0.0625 to 0.0625
- w_up: bfloat16 [8192, 14336], P('head', ('seq', 'rep')), may hold values from -0.0625 to 0.0625
- w_down: bfloat16 [14336, 8192], P(('seq', 'rep'), 'head'), may hold values from -0.046875 to 0.046875
- prefix_keys: bfloat16 [8192, 8, 128], P(('parts', 'seq', 'rep'), 'head'), may hold values from -500 to 500
- prompt_value_rows: bfloat16 [8192, 8, 128], P(('parts', 'seq', 'rep'), 'head'), may hold values from -6 to 6
- private_suffix_keys: bfloat16 [16, 128, 8, 128], P(('parts', 'seq', 'rep'), None, 'head'), may hold values from -21 to 21
- private_suffix_values: bfloat16 [16, 128, 8, 128], P(('parts', 'seq', 'rep'), None, 'head'), may hold values from -6 to 6
- suffix_lengths: int32 [16], P('parts'), may hold values from 1 to 128, 1024 in all
Outputs:
- mixed: bfloat16 [16, 8192], P(('parts', 'seq', 'rep'), 'head')
Inputs may be any that keep to these rules, and one draw needn't show every extreme that they name: Row r's suffix holds suffix_lengths[r] live tokens in its first slots; the lengths sum to 1024 and the largest is exactly 128.
All inputs are finite; a program needn't handle non-finite values.
Results may differ from a plain program's by a relative error of at most 0.024.
Values may be sent and summed in bfloat16 or wider, within the bound.
No kernel may reach another device: no remote copies, remote signals or barrier semaphores. Data moves between devices by JAX's collectives and lax.ppermute only.
A program may use at most 64 MiB of HBM per device.

v0:
```python
import functools
import math

import jax
import jax.numpy as jnp
from jax import lax
from jax.experimental import pallas as pl
from jax.experimental.pallas import tpu as pltpu
from jax.sharding import PartitionSpec as P


QUERY_HEADS = 64
KEY_VALUE_HEADS = 8
EPSILON = 1e-05
ROPE_BASE = 500000.0
LANES = ("seq", "rep")
ARRIVE_WORK, JOIN_WORK = 3_000_000_000, 1_000_000_000
F32 = jnp.float32
BF16 = jnp.bfloat16


def swap(x, axis, bit):
    size = lax.axis_size(axis)
    return lax.ppermute(x, axis, [(i, i ^ bit) for i in range(size)])


def bits_of(size):
    bit = 1
    while bit < size:
        yield bit
        bit *= 2


def lane_index():
    return lax.axis_index("seq") * lax.axis_size("rep") + lax.axis_index("rep")


def take(x, start, size, axis):
    return lax.dynamic_slice_in_dim(x, start, size, axis)


def in_order(flag, mine, other, axis):
    first = jnp.where(flag, other, mine)
    second = jnp.where(flag, mine, other)
    return jnp.concatenate([first, second], axis=axis)


def split_parts(value, count):
    parts = []
    for _ in range(count):
        head = lax.reduce_precision(value, 8, 7)
        parts.append(head)
        value = value - head
    return parts


def local_call(body, outs, *args, flops=3_000_000_000):
    return pl.pallas_call(
        body,
        out_shape=outs,
        in_specs=[pl.BlockSpec(memory_space=pltpu.VMEM)] * len(args),
        cost_estimate=pl.CostEstimate(flops=flops, bytes_accessed=0, transcendentals=0),
        compiler_params=pltpu.CompilerParams(vmem_limit_bytes=4 << 20),
    )(*args)


def add_kernel(total_ref, *refs):
    *got_refs, next_ref, send_ref = refs
    total = total_ref[...]
    for got_ref in got_refs:
        total = total + got_ref[...].astype(F32)
    next_ref[...] = total
    send_ref[...] = total.astype(BF16)


def add_stage(total, gots):
    shapes = (
        jax.ShapeDtypeStruct(total.shape, F32),
        jax.ShapeDtypeStruct(total.shape, BF16),
    )
    return local_call(add_kernel, shapes, total, *gots)


def rope_kernel(width, total_ref, cosine_ref, sine_ref, *refs):
    *got_refs, out_ref = refs
    total = total_ref[...]
    for got_ref in got_refs:
        total = total + got_ref[...].astype(F32)
    wide = out_ref.shape[1]
    squares = jnp.sum(total[:, wide:], axis=1, keepdims=True)
    inverse = lax.rsqrt(squares / width + EPSILON)
    cosine, sine = cosine_ref[...], sine_ref[...]
    size = cosine.shape[1]
    for first in range(0, wide, size):
        head = total[:, first : first + size] * inverse
        turned = head * cosine + pltpu.roll(head, size // 2, 1) * sine
        out_ref[:, first : first + size] = turned.astype(BF16)


def arrive_kernel(half_lanes, mine_ref, near_ref, far_ref, out_ref):
    home = lane_index() // half_lanes == lax.axis_index("head")
    other = jnp.where(home, mine_ref[...], far_ref[...])
    out_ref[...] = (near_ref[...].astype(F32) + other.astype(F32)).astype(BF16)


def arrive(half_lanes, mine, near, far):
    return local_call(
        functools.partial(arrive_kernel, half_lanes),
        jax.ShapeDtypeStruct(mine.shape, BF16),
        mine,
        near,
        far,
        flops=ARRIVE_WORK,
    )


def join_kernel(one_ref, two_ref, out_ref):
    cut = one_ref.shape[1]
    out_ref[:, :cut] = one_ref[...]
    out_ref[:, cut:] = two_ref[...]


def join(one, two):
    shape = (one.shape[0], one.shape[1] + two.shape[1])
    return local_call(join_kernel, jax.ShapeDtypeStruct(shape, BF16), one, two, flops=JOIN_WORK)


def parts_of(value, heads):
    lane = lax.broadcasted_iota(jnp.int32, value.shape, 1)
    value = jnp.where(lane < heads, value, 0.0)
    packed = jnp.zeros_like(value)
    for i in range(3):
        head = value.astype(BF16).astype(F32)
        packed = packed + (pltpu.roll(head, i * heads, 1) if i else head)
        value = value - head
    return packed


def joined(packed, heads):
    lanes = packed.shape[1]
    value = packed
    for i in range(1, 3):
        value = value + pltpu.roll(packed, lanes - i * heads, 1)
    return value


def merge_kernel(heads, size, last, out_ref, lse_ref, *refs):
    count = len(refs) - (1 if last else 3)
    got_refs, refs = refs[:count], refs[count:]
    wide = heads * size
    lses = [lse_ref[...]] + [joined(ref[:, wide:].astype(F32), heads) for ref in got_refs]
    high = functools.reduce(jnp.maximum, lses)
    weights = [jnp.exp(lse - high) for lse in lses]
    total = functools.reduce(jnp.add, weights)
    shares = [weight / total for weight in weights]
    for h in range(heads):
        cols = slice(h * size, (h + 1) * size)
        merged = shares[0][:, h : h + 1] * out_ref[:, cols]
        for share, ref in zip(shares[1:], got_refs):
            merged = merged + share[:, h : h + 1] * ref[:, cols].astype(F32)
        if last:
            refs[0][:, cols] = merged.astype(BF16)
        else:
            refs[0][:, cols] = merged
            refs[2][:, cols] = merged.astype(BF16)
    if not last:
        lse = high + jnp.log(total)
        refs[1][...] = lse
        refs[2][:, wide:] = parts_of(lse, heads).astype(BF16)


def merge_stage(state, gots, heads, size, last):
    out, lse = state
    rows = out.shape[0]
    wide = heads * size
    if last:
        outs = jax.ShapeDtypeStruct((rows, wide), BF16)
    else:
        outs = (
            jax.ShapeDtypeStruct((rows, wide), F32),
            jax.ShapeDtypeStruct(lse.shape, F32),
            jax.ShapeDtypeStruct((rows, wide + lse.shape[1]), BF16),
        )
    body = functools.partial(merge_kernel, heads, size, last)
    return local_call(body, outs, out, lse, *gots)


def rope_tables(positions, width):
    half = width // 2
    exponent = jnp.arange(half, dtype=F32) * (2.0 / width)
    frequency = jnp.exp(-math.log(ROPE_BASE) * exponent)
    angles = positions.astype(F32)[:, None] * frequency[None, :]
    cosine, sine = jnp.cos(angles), jnp.sin(angles)
    return jnp.concatenate([cosine, cosine], axis=1), jnp.concatenate([-sine, sine], axis=1)


def exchanges(size):
    bits = list(bits_of(size))
    if len(bits) < 2:
        return [[bit] for bit in bits]
    low, high = bits[-2:]
    return [[bit] for bit in bits[:-2]] + [[low, high, low | high]]


def merge(one, two):
    out_one, lse_one = one
    out_two, lse_two = two
    high = jnp.maximum(lse_one, lse_two)
    w_one = jnp.exp(lse_one - high)
    w_two = jnp.exp(lse_two - high)
    total = w_one + w_two
    out = out_one * (w_one / total)[..., None] + out_two * (w_two / total)[..., None]
    return out, high + jnp.log(total)


def pack(out, lse):
    rows, heads, size = out.shape
    parts = jnp.concatenate(split_parts(lse, 3), axis=1)
    pad = -parts.shape[1] % 128
    parts = jnp.pad(parts, ((0, 0), (0, pad)))
    return jnp.concatenate([out.reshape(rows, heads * size), parts], axis=1).astype(BF16)


def steps_of(size, most):
    step = min(size, most)
    while size % step or (step < size and step % 128):
        step -= 1
    return step


def weight_call(body, outs, weights, *args):
    count = len(weights)
    total = sum(weight.size * weight.dtype.itemsize for weight in weights)

    def kernel(*refs):
        body(refs[:count], *refs[count:])

    return pl.pallas_call(
        kernel,
        out_shape=outs,
        in_specs=[pl.BlockSpec(memory_space=pltpu.VMEM)] * (count + len(args)),
        cost_estimate=pl.CostEstimate(flops=0, bytes_accessed=total, transcendentals=0),
        compiler_params=pltpu.CompilerParams(vmem_limit_bytes=total + (4 << 20)),
    )(*weights, *args)


def seal_kernel(lanes, gained_ref, squares_ref, out_ref):
    local = gained_ref.shape[1]
    out_ref[:, :local] = gained_ref[...]
    squares = squares_ref[...]
    high = squares.astype(BF16).astype(F32)
    low = squares - high
    slot = lax.broadcasted_iota(jnp.int32, (squares.shape[0], out_ref.shape[1] - local), 1)
    lane = lane_index()
    tail = jnp.where(slot == lane, high, jnp.where(slot == lane + lanes, low, 0.0))
    out_ref[:, local:] = tail.astype(BF16)


def query_kernel(local, weights, *refs):
    *x_refs, mine_ref, give_ref = refs
    (weight,) = weights
    x = x_refs[0][...]
    if len(x_refs) == 2:
        other = x_refs[1][...]
        second = lax.axis_index("head") == 1
        x = jnp.concatenate([jnp.where(second, other, x), jnp.where(second, x, other)], axis=0)
    half = weight.shape[1] // 2
    upper = lax.axis_index("rep") == 1
    step = steps_of(half, 1024)
    for c in range(0, half, step):
        low = jnp.dot(x[:, :local], weight[:, c : c + step], preferred_element_type=F32)
        high = jnp.dot(
            x[:, :local], weight[:, half + c : half + c + step], preferred_element_type=F32
        )
        mine_ref[:, c : c + step] = jnp.where(upper, high, low)
        give_ref[:, c : c + step] = jnp.where(upper, low, high).astype(BF16)
    mine_ref[:, half:] = x[:, local:].astype(F32)
    give_ref[:, half:] = x[:, local:]


def output_kernel(weights, mine_ref, other_ref, steered_ref, out_ref):
    (weight,) = weights
    half = weight.shape[0] // 2
    step = steps_of(half, 1024)
    total = jnp.zeros(out_ref.shape, F32)
    upper = lax.axis_index("rep") == 1
    for k in range(0, half, step):
        cols = slice(k, k + step)
        mine, other = mine_ref[:, cols], other_ref[:, cols]
        low, high = jnp.where(upper, other, mine), jnp.where(upper, mine, other)
        total += jnp.dot(low, weight[k : k + step, :], preferred_element_type=F32)
        total += jnp.dot(high, weight[half + k : half + k + step, :], preferred_element_type=F32)
    block = steered_ref.shape[0]
    for g in range(out_ref.shape[0] // block):
        rows = slice(g * block, (g + 1) * block)
        own = jnp.where(lax.axis_index("head") == g, steered_ref[...], 0.0)
        out_ref[rows, :] = (total[rows] + own).astype(BF16)


def wide_kernel(local, places, weights, x_ref, gain_ref, *outs):
    gate, up, tail_ref, own_ref = outs
    wide = x_ref.shape[1]
    x = x_ref[...].astype(F32)
    squares = jnp.sum(x * x, axis=1, keepdims=True)
    lane = lax.broadcasted_iota(jnp.int32, tail_ref.shape, 1)
    tail_ref[...] = jnp.where(lane == 0, squares, 0.0)
    sums = [None] * len(weights)
    row = lax.broadcasted_iota(jnp.int32, (x.shape[0], local), 0)
    for b in range(wide // local):
        place = places(b)
        start = pl.multiple_of(place * local, local)
        whole = lax.axis_index("head") * weights[0].shape[0] + place * local
        scale = gain_ref[:, pl.ds(pl.multiple_of(whole, local), local)]
        block = x[:, b * local : (b + 1) * local]
        part = (block * scale).astype(BF16)
        for i in range(own_ref.shape[0]):
            own = jnp.where(row == lane_index() * own_ref.shape[0] + i, block, 0.0)
            own_ref[i : i + 1, pl.ds(start, local)] = jnp.sum(own, axis=0, keepdims=True)
        for n, weight in enumerate(weights):
            got = jnp.dot(part, weight[pl.ds(start, local), :], preferred_element_type=F32)
            sums[n] = got if sums[n] is None else sums[n] + got
    gate[...] = sums[0]
    up[...] = sums[1]


def wide_call(weights, places, local, share, x, gain):
    rows = x.shape[0]
    outs = [jax.ShapeDtypeStruct((rows, weights[0].shape[1]), F32)] * 2
    outs.append(jax.ShapeDtypeStruct((rows, 128), F32))
    outs.append(jax.ShapeDtypeStruct((share, x.shape[1]), F32))
    body = functools.partial(wide_kernel, local, places)
    return weight_call(body, tuple(outs), weights, x, gain)


def pack_kernel(gate_ref, up_ref, tail_ref, out_ref):
    cut = gate_ref.shape[1]
    out_ref[:, :cut] = gate_ref[...].astype(BF16)
    out_ref[:, cut : 2 * cut] = up_ref[...].astype(BF16)
    out_ref[:, 2 * cut :] = parts_of(tail_ref[...], 1).astype(BF16)


def combine_kernel(gate_ref, up_ref, tail_ref, got_ref, gate_out, up_out, tail_out):
    cut = gate_ref.shape[1]
    gate_out[...] = gate_ref[...] + got_ref[:, :cut].astype(F32)
    up_out[...] = up_ref[...] + got_ref[:, cut : 2 * cut].astype(F32)
    tail_out[...] = tail_ref[...] + joined(got_ref[:, 2 * cut :].astype(F32), 1)


def down_kernel(lanes, width, weights, gate_ref, up_ref, tail_ref, mine_ref, give_ref):
    (weight,) = weights
    rows, _ = gate_ref.shape
    inverse = lax.rsqrt(tail_ref[:, :1] / width + EPSILON)
    gate = gate_ref[...] * inverse
    up = up_ref[...] * inverse
    hidden = (gate / (1.0 + jnp.exp(-gate)) * up).astype(BF16)
    share = rows // lanes
    row = lax.broadcasted_iota(jnp.int32, (rows, rows), 0)
    source = lax.broadcasted_iota(jnp.int32, (rows, rows), 1)
    left, turned = row // share, jnp.zeros_like(row)
    for _ in range(lanes.bit_length() - 1):
        turned = turned * 2 + left % 2
        left = left // 2
    turned = turned * share + row % share
    order = (turned == source).astype(F32).astype(BF16)
    hidden = jnp.dot(order, hidden, preferred_element_type=F32).astype(BF16)
    half = rows // 2
    upper = lax.axis_index("rep") == 1
    step = steps_of(weight.shape[1], 1024)
    for c in range(0, weight.shape[1], step):
        cols = slice(c, c + step)
        block = jnp.dot(hidden, weight[:, cols], preferred_element_type=F32)
        low, high = block[:half], block[half:]
        mine_ref[:, cols] = jnp.where(upper, high, low)
        give_ref[:, cols] = jnp.where(upper, low, high).astype(BF16)


def shards(
    residual,
    coefficients,
    directions,
    attn_gain,
    mlp_gain,
    w_query,
    w_output,
    w_gate,
    w_up,
    w_down,
    prefix_keys,
    prompt_value_rows,
    private_suffix_keys,
    private_suffix_values,
    suffix_lengths,
):
    lanes = lax.axis_size(LANES)
    lane = lax.axis_index(LANES)
    rep = lax.axis_index("rep")
    seq_size = lax.axis_size("seq")
    groups = lax.axis_size("head")
    group = lax.axis_index("head")
    block_rows = residual.shape[0]
    rows = block_rows * groups
    share = rows // lanes
    first_own = lane * share
    width = w_gate.shape[0] * groups
    prompt_length = prefix_keys.shape[0] * lanes
    kv_local, size = prefix_keys.shape[1:]
    heads_per_group = QUERY_HEADS // KEY_VALUE_HEADS
    heads = kv_local * heads_per_group
    suffix_tokens = private_suffix_keys.shape[1]

    local = residual.shape[1]
    slots = 2 * lanes + (-2 * lanes % 128)
    steered = residual.astype(F32) + jnp.dot(
        coefficients, directions, precision=lax.Precision.HIGHEST
    )
    squares = jnp.sum(steered * steered, axis=1, keepdims=True)
    gained = local_call(
        functools.partial(seal_kernel, lanes),
        jax.ShapeDtypeStruct((block_rows, local + slots), BF16),
        (steered * attn_gain[None, :]).astype(BF16),
        squares,
    )
    if groups == 2:
        gained = (gained, swap(gained, "head", 1))
    else:
        gained = (lax.all_gather(gained, "head", axis=0, tiled=True),)

    columns = w_query.shape[1] // 2
    wide = columns + slots
    mine, give = weight_call(
        functools.partial(query_kernel, local),
        (jax.ShapeDtypeStruct((rows, wide), F32), jax.ShapeDtypeStruct((rows, wide), BF16)),
        (w_query,),
        *gained,
    )
    total = mine + swap(give, "rep", 1).astype(F32)
    send = total.astype(BF16)
    cosine, sine = rope_tables(prompt_length + suffix_lengths - 1, size)
    plan = exchanges(seq_size)
    for bits in plan[:-1]:
        total, send = add_stage(total, [swap(send, "seq", bit) for bit in bits])
    half_queries = local_call(
        functools.partial(rope_kernel, width),
        jax.ShapeDtypeStruct((rows, columns), BF16),
        total,
        cosine,
        sine,
        *[swap(send, "seq", bit) for bit in plan[-1]],
    )
    queries = in_order(rep == 1, half_queries, swap(half_queries, "rep", 1), 1)
    queries = queries.reshape(rows, kv_local, heads_per_group, size)

    scale = 1.0 / math.sqrt(size)
    scores = (
        jnp.einsum("rkgd,pkd->rkgp", queries, prefix_keys, preferred_element_type=F32) * scale
    )
    highest = jnp.max(scores, axis=3)
    weights = jnp.exp(scores - highest[..., None])
    totals = jnp.sum(weights, axis=3)
    weighted = jnp.einsum(
        "rkgp,pkd->rkgd", weights.astype(BF16), prompt_value_rows, preferred_element_type=F32
    )
    prefix_out = (weighted / totals[..., None]).reshape(rows, heads, size)
    prefix_lse = (highest + jnp.log(totals)).reshape(rows, heads)
    own_queries = take(queries, first_own, share, 0)
    own_lengths = take(suffix_lengths, first_own, share, 0)
    live = (jnp.arange(suffix_tokens)[None, :] < own_lengths[:, None])[:, None, None, :]
    tail_scores = (
        jnp.einsum(
            "rkgd,rskd->rkgs", own_queries, private_suffix_keys, preferred_element_type=F32
        )
        * scale
    )
    tail_scores = jnp.where(live, tail_scores, -jnp.inf)
    tail_high = jnp.max(tail_scores, axis=3)
    tail_weights = jnp.where(live, jnp.exp(tail_scores - tail_high[..., None]), 0.0)
    tail_totals = jnp.sum(tail_weights, axis=3)
    tail_weighted = jnp.einsum(
        "rkgs,rskd->rkgd",
        tail_weights.astype(BF16),
        private_suffix_values,
        preferred_element_type=F32,
    )
    tail_out = (tail_weighted / tail_totals[..., None]).reshape(share, heads, size)
    tail_lse = (tail_high + jnp.log(tail_totals)).reshape(share, heads)
    own_out = take(prefix_out, first_own, share, 0)
    own_lse = take(prefix_lse, first_own, share, 0)
    own_out, own_lse = merge((own_out, own_lse), (tail_out, tail_lse))
    prefix_out = lax.dynamic_update_slice_in_dim(prefix_out, own_out, first_own, 0)
    prefix_lse = lax.dynamic_update_slice_in_dim(prefix_lse, own_lse, first_own, 0)

    half_heads = heads // 2
    state = (
        take(prefix_out, rep * half_heads, half_heads, 1),
        take(prefix_lse, rep * half_heads, half_heads, 1),
    )
    give = pack(
        take(prefix_out, (1 - rep) * half_heads, half_heads, 1),
        take(prefix_lse, (1 - rep) * half_heads, half_heads, 1),
    )
    out, lse = state
    lse = jnp.pad(lse, ((0, 0), (0, 128 - half_heads)))
    state = (out.reshape(rows, half_heads * size), lse)
    gots = [swap(give, "rep", 1)]
    for bits in plan:
        *state, send = merge_stage(state, gots, half_heads, size, False)
        gots = [swap(send, "seq", bit) for bit in bits]
    attended = merge_stage(state, gots, half_heads, size, True)

    other = swap(attended, "rep", 1)
    middle = weight_call(
        output_kernel,
        jax.ShapeDtypeStruct((rows, local), BF16),
        (w_output,),
        attended,
        other,
        steered,
    )

    shard_width = width // groups
    weights = (w_gate, w_up)
    gain = mlp_gain[None, :]
    if groups == 2 and seq_size >= 2:
        half = seq_size // 2
        near, far = [], []
        for s in range(seq_size):
            g = s // half
            near.append((2 * s + 1 - g, 2 * s + g))
            near.append((2 * s + g, 2 * (s ^ half) + g))
            far.append((2 * s + 1 - g, 2 * (s ^ half) + g))
        got = lax.ppermute(middle, ("seq", "head"), near)
        away = lax.ppermute(middle, ("seq", "head"), far)
        middle = arrive(lanes // 2, middle, got, away)
        stages = [("seq", bit) for bit in sorted(bits_of(half), reverse=True)] + [("rep", 1)]
        turns = [0]
        for axis, bit in stages:
            middle = join(middle, swap(middle, axis, bit))
            turns += [turn ^ (1 if axis == "rep" else 2 * bit) for turn in turns]

        def places(b):
            return (lane_index() % (lanes // 2)) ^ turns[b]

    else:
        for bit in bits_of(groups):
            middle = (middle.astype(F32) + swap(middle, "head", bit).astype(F32)).astype(BF16)
        middle = lax.all_gather(middle, LANES, axis=1, tiled=True)
        middle = take(middle, group * shard_width, shard_width, 1)

        def places(b):
            return b

    gate, up, tail, own_middle = wide_call(weights, places, local, share, middle, gain)

    ff_local = w_gate.shape[1]
    for bit in bits_of(groups):
        send = local_call(
            pack_kernel, jax.ShapeDtypeStruct((rows, 2 * ff_local + 128), BF16), gate, up, tail
        )
        got = swap(send, "head", bit)
        shapes = tuple(jax.ShapeDtypeStruct(x.shape, F32) for x in (gate, up, tail))
        gate, up, tail = local_call(combine_kernel, shapes, gate, up, tail, got)
    half_rows = rows // 2
    down, give = weight_call(
        functools.partial(down_kernel, lanes, width),
        (
            jax.ShapeDtypeStruct((half_rows, shard_width), F32),
            jax.ShapeDtypeStruct((half_rows, shard_width), BF16),
        ),
        (w_down,),
        gate,
        up,
        tail,
    )
    down = down + swap(give, "rep", 1).astype(F32)
    size_left = half_rows
    bits = list(bits_of(seq_size))
    seq = lax.axis_index("seq")
    for bit in bits[:-2]:
        size_left //= 2
        upper = (seq & bit) != 0
        low, high = down[:size_left], down[size_left:]
        got = swap(jnp.where(upper, low, high).astype(BF16), "seq", bit)
        down = jnp.where(upper, high, low) + got.astype(F32)
    unit = bits[-2]
    quarters = down.reshape(2, 2, share, shard_width)

    def quarter(place):
        one, two = place // unit % 2, place // (2 * unit) % 2
        part = lax.dynamic_index_in_dim(quarters, one, 0, keepdims=False)
        return lax.dynamic_index_in_dim(part, two, 0, keepdims=False)

    down = quarter(seq)
    gots = [
        swap(quarter(seq ^ bit).astype(BF16), "seq", bit)
        for bit in (unit, 2 * unit, 3 * unit)
    ]
    for got in gots:
        down = down + got.astype(F32)
    return (own_middle + down).astype(BF16)


def solution(mesh):
    return jax.shard_map(
        shards,
        mesh=mesh,
        in_specs=(
            P(("parts", "head"), ("seq", "rep")),
            P(("parts", "head"), None),
            P(None, ("seq", "rep")),
            P(("seq", "rep")),
            P(),
            P(("seq", "rep"), "head"),
            P("head", ("seq", "rep")),
            P("head", ("seq", "rep")),
            P("head", ("seq", "rep")),
            P(("seq", "rep"), "head"),
            P(("parts", "seq", "rep"), "head", None),
            P(("parts", "seq", "rep"), "head", None),
            P(("parts", "seq", "rep"), None, "head", None),
            P(("parts", "seq", "rep"), None, "head", None),
            P("parts"),
        ),
        out_specs=P(("parts", "seq", "rep"), "head"),
        check_vma=False,
    )
```

profile of v0, /device:TPU:0, one launch (start us, length us, event | category | flops | bytes accessed | tf_op | source)
XLA Modules:
  0.0 82.7 jit_solution(3799877534853932398)
XLA Ops:
  1.3 3.0 %collective-permute-start = (bf16[8,640]{1,0:T(8,128)(2,1)S(1)}, bf16[8,640]{1,0:T(8,128)(2,1)S(1)}, u32[]{:S(2)}, u32[]{:S(2)}) collective-permute-start(bf16[8,640]{1,0:T(8,128)(2,1)S(1)} %shard_map.145.refs_1_), channel_id=1, source_target_pairs={{0,2},{2,0},{1,3},{3,1},{4,6},{6,4},{5,7},{7,5},{8,10},{10,8},{9,1... | collective-permute-start | bytes 30728 | tf_op jit(solution)/shard_map/ppermute | solution.py:24
  4.2 1.6 %collective-permute-done.refs_2_ = bf16[8,640]{1,0:T(8,128)(2,1)S(1)} collective-permute-done((bf16[8,640]{1,0:T(8,128)(2,1)S(1)}, bf16[8,640]{1,0:T(8,128)(2,1)S(1)}, u32[]{:S(2)}, u32[]{:S(2)}) %collective-permute-start) | collective-permute-done | bytes 10272 | tf_op jit(solution)/shard_map/ppermute | solution.py:24
  6.6 1.2 %collective-permute-done.1 = bf16[16,2176]{1,0:T(8,128)(2,1)S(1)} collective-permute-done((bf16[16,2176]{1,0:T(8,128)(2,1)S(1)}, bf16[16,2176]{1,0:T(8,128)(2,1)S(1)}, u32[]{:S(2)}, u32[]{:S(2)}) %collective-permute-start.1) | collective-permute-done | bytes 69664 | tf_op jit(solution)/shard_map/ppermute | solution.py:24
  7.8 2.1 %collective-permute-start.2 = (bf16[16,2176]{1,0:T(8,128)(2,1)S(1)}, bf16[16,2176]{1,0:T(8,128)(2,1)S(1)}, u32[]{:S(2)}, u32[]{:S(2)}) collective-permute-start(bf16[16,2176]{1,0:T(8,128)(2,1)S(1)} %get-tuple-element.46), channel_id=1, source_target_pairs={{0,4},{4,0},{8,12},{12,8},{16,20},{20,16},{24,28},{28,24},{1,5},{5... | collective-permute-start | bytes 208904 | tf_op jit(solution)/shard_map/ppermute | solution.py:24
  10.7 1.8 %collective-permute-done.2.refs_0_ = bf16[16,2176]{1,0:T(8,128)(2,1)S(1)} collective-permute-done((bf16[16,2176]{1,0:T(8,128)(2,1)S(1)}, bf16[16,2176]{1,0:T(8,128)(2,1)S(1)}, u32[]{:S(2)}, u32[]{:S(2)}) %collective-permute-start.2) | collective-permute-done | bytes 69664 | tf_op jit(solution)/shard_map/ppermute | solution.py:24
  12.5 4.0 %collective-permute-start.5 = (bf16[16,2176]{1,0:T(8,128)(2,1)S(1)}, bf16[16,2176]{1,0:T(8,128)(2,1)S(1)}, u32[]{:S(2)}, u32[]{:S(2)}) collective-permute-start(bf16[16,2176]{1,0:T(8,128)(2,1)S(1)} %get-tuple-element.27), channel_id=1, source_target_pairs={{0,24},{4,28},{8,16},{12,20},{16,8},{20,12},{24,0},{28,4},{1,25},{... | collective-permute-start | bytes 208904 | tf_op jit(solution)/shard_map/ppermute | solution.py:24
  17.2 2.1 %collective-permute-done.5.refs_2_ = bf16[16,2176]{1,0:T(8,128)(2,1)S(1)} collective-permute-done((bf16[16,2176]{1,0:T(8,128)(2,1)S(1)}, bf16[16,2176]{1,0:T(8,128)(2,1)S(1)}, u32[]{:S(2)}, u32[]{:S(2)}) %collective-permute-start.5) | collective-permute-done | bytes 69664 | tf_op jit(solution)/shard_map/ppermute | solution.py:24
  19.3 2.6 %collective-permute-done.4.refs_1_ = bf16[16,2176]{1,0:T(8,128)(2,1)S(1)} collective-permute-done((bf16[16,2176]{1,0:T(8,128)(2,1)S(1)}, bf16[16,2176]{1,0:T(8,128)(2,1)S(1)}, u32[]{:S(2)}, u32[]{:S(2)}) %collective-permute-start.4) | collective-permute-done | bytes 69664 | tf_op jit(solution)/shard_map/ppermute | solution.py:24
  27.5 1.6 %collective-permute-start.8 = (bf16[16,2176]{1,0:T(8,128)(2,1)S(1)}, bf16[16,2176]{1,0:T(8,128)(2,1)S(1)}, u32[]{:S(2)}, u32[]{:S(2)}) collective-permute-start(bf16[16,2176]{1,0:T(8,128)(2,1)S(1)} %get-tuple-element.30), channel_id=1, source_target_pairs={{0,4},{4,0},{8,12},{12,8},{16,20},{20,16},{24,28},{28,24},{1,5},{5... | collective-permute-start | bytes 208904 | tf_op jit(solution)/shard_map/ppermute | solution.py:24
  29.1 2.8 %collective-permute-done.8.refs_0_ = bf16[16,2176]{1,0:T(8,128)(2,1)S(1)} collective-permute-done((bf16[16,2176]{1,0:T(8,128)(2,1)S(1)}, bf16[16,2176]{1,0:T(8,128)(2,1)S(1)}, u32[]{:S(2)}, u32[]{:S(2)}) %collective-permute-start.8) | collective-permute-done | bytes 69664 | tf_op jit(solution)/shard_map/ppermute | solution.py:24
  32.1 2.6 %collective-permute-start.11 = (bf16[16,2176]{1,0:T(8,128)(2,1)S(1)}, bf16[16,2176]{1,0:T(8,128)(2,1)S(1)}, u32[]{:S(2)}, u32[]{:S(2)}) collective-permute-start(bf16[16,2176]{1,0:T(8,128)(2,1)S(1)} %get-tuple-element.33), channel_id=1, source_target_pairs={{0,24},{4,28},{8,16},{12,20},{16,8},{20,12},{24,0},{28,4},{1,25},{... | collective-permute-start | bytes 208904 | tf_op jit(solution)/shard_map/ppermute | solution.py:24
  34.7 1.9 %collective-permute-start.9 = (bf16[16,2176]{1,0:T(8,128)(2,1)S(1)}, bf16[16,2176]{1,0:T(8,128)(2,1)S(1)}, u32[]{:S(2)}, u32[]{:S(2)}) collective-permute-start(bf16[16,2176]{1,0:T(8,128)(2,1)S(1)} %get-tuple-element.33), channel_id=1, source_target_pairs={{0,8},{4,12},{8,0},{12,4},{16,24},{20,28},{24,16},{28,20},{1,9},{5... | collective-permute-start | bytes 208904 | tf_op jit(solution)/shard_map/ppermute | solution.py:24
  36.6 2.0 %collective-permute-done.11.refs_2_ = bf16[16,2176]{1,0:T(8,128)(2,1)S(1)} collective-permute-done((bf16[16,2176]{1,0:T(8,128)(2,1)S(1)}, bf16[16,2176]{1,0:T(8,128)(2,1)S(1)}, u32[]{:S(2)}, u32[]{:S(2)}) %collective-permute-start.11) | collective-permute-done | bytes 69664 | tf_op jit(solution)/shard_map/ppermute | solution.py:24
  38.5 2.3 %collective-permute-done.10.refs_1_ = bf16[16,2176]{1,0:T(8,128)(2,1)S(1)} collective-permute-done((bf16[16,2176]{1,0:T(8,128)(2,1)S(1)}, bf16[16,2176]{1,0:T(8,128)(2,1)S(1)}, u32[]{:S(2)}, u32[]{:S(2)}) %collective-permute-start.10) | collective-permute-done | bytes 69664 | tf_op jit(solution)/shard_map/ppermute | solution.py:24
  41.2 1.2 %collective-permute-done.12.refs_2_ = bf16[16,2048]{1,0:T(8,128)(2,1)S(1)} collective-permute-done((bf16[16,2048]{1,0:T(8,128)(2,1)S(1)}, bf16[16,2048]{1,0:T(8,128)(2,1)S(1)}, u32[]{:S(2)}, u32[]{:S(2)}) %collective-permute-start.12) | collective-permute-done | bytes 65568 | tf_op jit(solution)/shard_map/ppermute | solution.py:24
  43.8 5.2 %collective-permute-start.13 = (bf16[16,512]{1,0:T(8,128)(2,1)S(1)}, bf16[16,512]{1,0:T(8,128)(2,1)S(1)}, u32[]{:S(2)}, u32[]{:S(2)}) collective-permute-start(bf16[16,512]{1,0:T(8,128)(2,1)S(1)} %shard_map.152.mine_ref), channel_id=1, source_target_pairs={{2,0},{0,16},{6,4},{4,20},{10,8},{8,24},{14,12},{12,28},{16,18},{1... | collective-permute-start | bytes 49160 | tf_op jit(solution)/shard_map/ppermute | solution.py:531
  48.9 1.4 %collective-permute-done.13.near_ref = bf16[16,512]{1,0:T(8,128)(2,1)S(1)} collective-permute-done((bf16[16,512]{1,0:T(8,128)(2,1)S(1)}, bf16[16,512]{1,0:T(8,128)(2,1)S(1)}, u32[]{:S(2)}, u32[]{:S(2)}) %collective-permute-start.13) | collective-permute-done | bytes 16416 | tf_op jit(solution)/shard_map/ppermute | solution.py:531
  51.4 2.8 %collective-permute-done.15.two_ref = bf16[16,512]{1,0:T(8,128)(2,1)S(1)} collective-permute-done((bf16[16,512]{1,0:T(8,128)(2,1)S(1)}, bf16[16,512]{1,0:T(8,128)(2,1)S(1)}, u32[]{:S(2)}, u32[]{:S(2)}) %collective-permute-start.15) | collective-permute-done | bytes 16416 | tf_op jit(solution)/shard_map/ppermute | solution.py:24
  54.2 1.5 %collective-permute-start.16 = (bf16[16,1024]{1,0:T(8,128)(2,1)S(1)}, bf16[16,1024]{1,0:T(8,128)(2,1)S(1)}, u32[]{:S(2)}, u32[]{:S(2)}) collective-permute-start(bf16[16,1024]{1,0:T(8,128)(2,1)S(1)} %shard_map.154.one_ref), channel_id=1, source_target_pairs={{0,4},{4,0},{8,12},{12,8},{16,20},{20,16},{24,28},{28,24},{1,5},{5... | collective-permute-start | bytes 98312 | tf_op jit(solution)/shard_map/ppermute | solution.py:24
  55.8 2.4 %collective-permute-done.16.two_ref = bf16[16,1024]{1,0:T(8,128)(2,1)S(1)} collective-permute-done((bf16[16,1024]{1,0:T(8,128)(2,1)S(1)}, bf16[16,1024]{1,0:T(8,128)(2,1)S(1)}, u32[]{:S(2)}, u32[]{:S(2)}) %collective-permute-start.16) | collective-permute-done | bytes 32800 | tf_op jit(solution)/shard_map/ppermute | solution.py:24
  58.2 1.2 %collective-permute-done.17.two_ref = bf16[16,2048]{1,0:T(8,128)(2,1)S(1)} collective-permute-done((bf16[16,2048]{1,0:T(8,128)(2,1)S(1)}, bf16[16,2048]{1,0:T(8,128)(2,1)S(1)}, u32[]{:S(2)}, u32[]{:S(2)}) %collective-permute-start.17) | collective-permute-done | bytes 65568 | tf_op jit(solution)/shard_map/ppermute | solution.py:24
  59.5 2.0 %shard_map.157 = (f32[16,896]{1,0:T(8,128)S(1)}, f32[16,896]{1,0:T(8,128)S(1)}, f32[16,128]{1,0:T(8,128)S(1)}, f32[1,4096]{1,0:T(1,128)S(1)}) custom-call(bf16[4096,896]{1,0:T(8,128)(2,1)S(1)} %bitcast.66, bf16[4096,896]{1,0:T(8,128)(2,1)S(1)} %bitcast.68, bf16[16,4096]{1,0:T(8,128)(2,1)S(1)} %shard_map.156.refs_2_, f32[1,8192]{1,0:T(1,128)S(1)} %bitcast.72), custom_call_target="tpu_custom_call" | custom-call | bytes 14680064 | tf_op jit(solution)/shard_map/pallas_call | solution.py:238
  61.6 1.9 %collective-permute-start.18 = (bf16[16,1920]{1,0:T(8,128)(2,1)S(1)}, bf16[16,1920]{1,0:T(8,128)(2,1)S(1)}, u32[]{:S(2)}, u32[]{:S(2)}) collective-permute-start(bf16[16,1920]{1,0:T(8,128)(2,1)S(1)} %shard_map.158), channel_id=1, source_target_pairs={{0,2},{2,0},{1,3},{3,1},{4,6},{6,4},{5,7},{7,5},{8,10},{10,8},{9,1... | collective-permute-start | bytes 184328 | tf_op jit(solution)/shard_map/ppermute | solution.py:24
  63.6 2.3 %collective-permute-done.18.got_ref = bf16[16,1920]{1,0:T(8,128)(2,1)S(1)} collective-permute-done((bf16[16,1920]{1,0:T(8,128)(2,1)S(1)}, bf16[16,1920]{1,0:T(8,128)(2,1)S(1)}, u32[]{:S(2)}, u32[]{:S(2)}) %collective-permute-start.18) | collective-permute-done | bytes 61472 | tf_op jit(solution)/shard_map/ppermute | solution.py:24
  66.0 1.2 %shard_map.160 = (f32[8,4096]{1,0:T(8,128)S(1)}, bf16[8,4096]{1,0:T(8,128)(2,1)S(1)}) custom-call(bf16[896,4096]{1,0:T(8,128)(2,1)S(1)} %bitcast.70, f32[16,896]{1,0:T(8,128)S(1)} %get-tuple-element.38.refs_1_, f32[16,896]{1,0:T(8,128)S(1)} %get-tuple-element.39.refs_2_, f32[16,128]{1,0:T(8,128)S(1)} %get-tuple-element.40.refs_3_), custom_call_target="tpu_custom_call" | custom-call | bytes 7340032 | tf_op jit(solution)/shard_map/pallas_call | solution.py:238
  67.2 1.3 %collective-permute-done.19 = bf16[8,4096]{1,0:T(8,128)(2,1)S(1)} collective-permute-done((bf16[8,4096]{1,0:T(8,128)(2,1)S(1)}, bf16[8,4096]{1,0:T(8,128)(2,1)S(1)}, u32[]{:S(2)}, u32[]{:S(2)}) %collective-permute-start.19) | collective-permute-done | bytes 65568 | tf_op jit(solution)/shard_map/ppermute | solution.py:24
  68.5 1.6 %collective-permute-start.20 = (bf16[4,4096]{1,0:T(4,128)(2,1)S(1)}, bf16[4,4096]{1,0:T(4,128)(2,1)S(1)}, u32[]{:S(2)}, u32[]{:S(2)}) collective-permute-start(bf16[4,4096]{1,0:T(4,128)(2,1)S(1)} %select_convert_fusion), channel_id=1, source_target_pairs={{0,4},{4,0},{8,12},{12,8},{16,20},{20,16},{24,28},{28,24},{1,5},{5... | collective-permute-start | bytes 98312 | tf_op jit(solution)/shard_map/ppermute | solution.py:24
  70.1 2.4 %collective-permute-done.20 = bf16[4,4096]{1,0:T(4,128)(2,1)S(1)} collective-permute-done((bf16[4,4096]{1,0:T(4,128)(2,1)S(1)}, bf16[4,4096]{1,0:T(4,128)(2,1)S(1)}, u32[]{:S(2)}, u32[]{:S(2)}) %collective-permute-start.20) | collective-permute-done | bytes 32800 | tf_op jit(solution)/shard_map/ppermute | solution.py:24
  72.7 2.0 %collective-permute-start.21 = (bf16[1,4096]{1,0:T(2,128)(2,1)S(1)}, bf16[1,4096]{1,0:T(2,128)(2,1)S(1)}, u32[]{:S(2)}, u32[]{:S(2)}) collective-permute-start(bf16[1,4096]{1,0:T(2,128)(2,1)S(1)} %get-tuple-element.50), channel_id=1, source_target_pairs={{0,8},{4,12},{8,0},{12,4},{16,24},{20,28},{24,16},{28,20},{1,9},{5... | collective-permute-start | bytes 24584 | tf_op jit(solution)/shard_map/ppermute | solution.py:24
  74.7 2.7 %collective-permute-start.23 = (bf16[1,4096]{1,0:T(2,128)(2,1)S(1)}, bf16[1,4096]{1,0:T(2,128)(2,1)S(1)}, u32[]{:S(2)}, u32[]{:S(2)}) collective-permute-start(bf16[1,4096]{1,0:T(2,128)(2,1)S(1)} %get-tuple-element.51), channel_id=1, source_target_pairs={{0,24},{4,28},{8,16},{12,20},{16,8},{20,12},{24,0},{28,4},{1,25},{... | collective-permute-start | bytes 24584 | tf_op jit(solution)/shard_map/ppermute | solution.py:24
  77.4 2.8 %collective-permute-done.23 = bf16[1,4096]{1,0:T(2,128)(2,1)S(1)} collective-permute-done((bf16[1,4096]{1,0:T(2,128)(2,1)S(1)}, bf16[1,4096]{1,0:T(2,128)(2,1)S(1)}, u32[]{:S(2)}, u32[]{:S(2)}) %collective-permute-start.23) | collective-permute-done | bytes 8224 | tf_op jit(solution)/shard_map/ppermute | solution.py:24
  80.2 1.8 %collective-permute-done.22 = bf16[1,4096]{1,0:T(2,128)(2,1)S(1)} collective-permute-done((bf16[1,4096]{1,0:T(2,128)(2,1)S(1)}, bf16[1,4096]{1,0:T(2,128)(2,1)S(1)}, u32[]{:S(2)}, u32[]{:S(2)}) %collective-permute-start.22) | collective-permute-done | bytes 8224 | tf_op jit(solution)/shard_map/ppermute | solution.py:24
  (104 shorter events, 12.9 us)
Async XLA Ops:
  0.0 24.0 %copy-start = (bf16[512,4,128]{2,1,0:T(4,128)(2,1)S(1)}, bf16[512,4,128]{2,1,0:T(4,128)(2,1)}, u32[]{:S(2)}) copy-start(bf16[512,4,128]{2,1,0:T(4,128)(2,1)} %param.25) | copy-start | bytes 1572868
  1.3 4.6 %collective-permute-start = (bf16[8,640]{1,0:T(8,128)(2,1)S(1)}, bf16[8,640]{1,0:T(8,128)(2,1)S(1)}, u32[]{:S(2)}, u32[]{:S(2)}) collective-permute-start(bf16[8,640]{1,0:T(8,128)(2,1)S(1)} %shard_map.145.refs_1_), channel_id=1, source_target_pairs={{0,2},{2,0},{1,3},{3,1},{4,6},{6,4},{5,7},{7,5},{8,10},{10,8},{9,1... | collective-permute-start | bytes 30728 | tf_op jit(solution)/shard_map/ppermute | solution.py:24
  6.5 1.3 %collective-permute-start.1 = (bf16[16,2176]{1,0:T(8,128)(2,1)S(1)}, bf16[16,2176]{1,0:T(8,128)(2,1)S(1)}, u32[]{:S(2)}, u32[]{:S(2)}) collective-permute-start(bf16[16,2176]{1,0:T(8,128)(2,1)S(1)} %get-tuple-element.25), channel_id=1, source_target_pairs={{0,1},{1,0},{2,3},{3,2},{4,5},{5,4},{6,7},{7,6},{8,9},{9,8},{10,11... | collective-permute-start | bytes 208904 | tf_op jit(solution)/shard_map/ppermute | solution.py:24
  7.8 4.6 %collective-permute-start.2 = (bf16[16,2176]{1,0:T(8,128)(2,1)S(1)}, bf16[16,2176]{1,0:T(8,128)(2,1)S(1)}, u32[]{:S(2)}, u32[]{:S(2)}) collective-permute-start(bf16[16,2176]{1,0:T(8,128)(2,1)S(1)} %get-tuple-element.46), channel_id=1, source_target_pairs={{0,4},{4,0},{8,12},{12,8},{16,20},{20,16},{24,28},{28,24},{1,5},{5... | collective-permute-start | bytes 208904 | tf_op jit(solution)/shard_map/ppermute | solution.py:24
  12.5 11.0 %copy-start.4 = (bf16[1,128,4,128]{3,2,1,0:T(4,128)(2,1)S(1)}, bf16[1,128,4,128]{3,2,1,0:T(4,128)(2,1)}, u32[]{:S(2)}) copy-start(bf16[1,128,4,128]{3,2,1,0:T(4,128)(2,1)} %param.27) | copy-start | bytes 393220
  12.5 6.8 %collective-permute-start.5 = (bf16[16,2176]{1,0:T(8,128)(2,1)S(1)}, bf16[16,2176]{1,0:T(8,128)(2,1)S(1)}, u32[]{:S(2)}, u32[]{:S(2)}) collective-permute-start(bf16[16,2176]{1,0:T(8,128)(2,1)S(1)} %get-tuple-element.27), channel_id=1, source_target_pairs={{0,24},{4,28},{8,16},{12,20},{16,8},{20,12},{24,0},{28,4},{1,25},{... | collective-permute-start | bytes 208904 | tf_op jit(solution)/shard_map/ppermute | solution.py:24
  16.4 5.5 %collective-permute-start.4 = (bf16[16,2176]{1,0:T(8,128)(2,1)S(1)}, bf16[16,2176]{1,0:T(8,128)(2,1)S(1)}, u32[]{:S(2)}, u32[]{:S(2)}) collective-permute-start(bf16[16,2176]{1,0:T(8,128)(2,1)S(1)} %get-tuple-element.27), channel_id=1, source_target_pairs={{0,16},{4,20},{8,24},{12,28},{16,0},{20,4},{24,8},{28,12},{1,17},{... | collective-permute-start | bytes 208904 | tf_op jit(solution)/shard_map/ppermute | solution.py:24
  16.5 5.5 %collective-permute-start.3 = (bf16[16,2176]{1,0:T(8,128)(2,1)S(1)}, bf16[16,2176]{1,0:T(8,128)(2,1)S(1)}, u32[]{:S(2)}, u32[]{:S(2)}) collective-permute-start(bf16[16,2176]{1,0:T(8,128)(2,1)S(1)} %get-tuple-element.27), channel_id=1, source_target_pairs={{0,8},{4,12},{8,0},{12,4},{16,24},{20,28},{24,16},{28,20},{1,9},{5... | collective-permute-start | bytes 208904 | tf_op jit(solution)/shard_map/ppermute | solution.py:24
  22.1 1.3 %collective-permute-start.6 = (bf16[16,2048]{1,0:T(8,128)(2,1)S(1)}, bf16[16,2048]{1,0:T(8,128)(2,1)S(1)}, u32[]{:S(2)}, u32[]{:S(2)}) collective-permute-start(bf16[16,2048]{1,0:T(8,128)(2,1)S(1)} %shard_map.148), channel_id=1, source_target_pairs={{0,1},{1,0},{2,3},{3,2},{4,5},{5,4},{6,7},{7,6},{8,9},{9,8},{10,11... | collective-permute-start | bytes 196616 | tf_op jit(solution)/shard_map/ppermute | solution.py:24
  25.9 1.3 %collective-permute-start.7 = (bf16[16,2176]{1,0:T(8,128)(2,1)S(1)}, bf16[16,2176]{1,0:T(8,128)(2,1)S(1)}, u32[]{:S(2)}, u32[]{:S(2)}) collective-permute-start(bf16[16,2176]{1,0:T(8,128)(2,1)S(1)} %pad_maximum_fusion), channel_id=1, source_target_pairs={{0,1},{1,0},{2,3},{3,2},{4,5},{5,4},{6,7},{7,6},{8,9},{9,8},{10,11... | collective-permute-start | bytes 208904 | tf_op jit(solution)/shard_map/ppermute | solution.py:24
  27.5 4.4 %collective-permute-start.8 = (bf16[16,2176]{1,0:T(8,128)(2,1)S(1)}, bf16[16,2176]{1,0:T(8,128)(2,1)S(1)}, u32[]{:S(2)}, u32[]{:S(2)}) collective-permute-start(bf16[16,2176]{1,0:T(8,128)(2,1)S(1)} %get-tuple-element.30), channel_id=1, source_target_pairs={{0,4},{4,0},{8,12},{12,8},{16,20},{20,16},{24,28},{28,24},{1,5},{5... | collective-permute-start | bytes 208904 | tf_op jit(solution)/shard_map/ppermute | solution.py:24
  32.1 10.4 %copy-start.2 = (bf16[4096,512]{1,0:T(8,128)(2,1)S(1)}, bf16[4096,512]{1,0:T(8,128)(2,1)}, u32[]{:S(2)}) copy-start(bf16[4096,512]{1,0:T(8,128)(2,1)} %refs_0_.5) | copy-start | bytes 12582916
  32.1 6.4 %collective-permute-start.11 = (bf16[16,2176]{1,0:T(8,128)(2,1)S(1)}, bf16[16,2176]{1,0:T(8,128)(2,1)S(1)}, u32[]{:S(2)}, u32[]{:S(2)}) collective-permute-start(bf16[16,2176]{1,0:T(8,128)(2,1)S(1)} %get-tuple-element.33), channel_id=1, source_target_pairs={{0,24},{4,28},{8,16},{12,20},{16,8},{20,12},{24,0},{28,4},{1,25},{... | collective-permute-start | bytes 208904 | tf_op jit(solution)/shard_map/ppermute | solution.py:24
  34.7 6.1 %collective-permute-start.10 = (bf16[16,2176]{1,0:T(8,128)(2,1)S(1)}, bf16[16,2176]{1,0:T(8,128)(2,1)S(1)}, u32[]{:S(2)}, u32[]{:S(2)}) collective-permute-start(bf16[16,2176]{1,0:T(8,128)(2,1)S(1)} %get-tuple-element.33), channel_id=1, source_target_pairs={{0,16},{4,20},{8,24},{12,28},{16,0},{20,4},{24,8},{28,12},{1,17},{... | collective-permute-start | bytes 208904 | tf_op jit(solution)/shard_map/ppermute | solution.py:24
  34.7 6.1 %collective-permute-start.9 = (bf16[16,2176]{1,0:T(8,128)(2,1)S(1)}, bf16[16,2176]{1,0:T(8,128)(2,1)S(1)}, u32[]{:S(2)}, u32[]{:S(2)}) collective-permute-start(bf16[16,2176]{1,0:T(8,128)(2,1)S(1)} %get-tuple-element.33), channel_id=1, source_target_pairs={{0,8},{4,12},{8,0},{12,4},{16,24},{20,28},{24,16},{28,20},{1,9},{5... | collective-permute-start | bytes 208904 | tf_op jit(solution)/shard_map/ppermute | solution.py:24
  41.1 1.3 %collective-permute-start.12 = (bf16[16,2048]{1,0:T(8,128)(2,1)S(1)}, bf16[16,2048]{1,0:T(8,128)(2,1)S(1)}, u32[]{:S(2)}, u32[]{:S(2)}) collective-permute-start(bf16[16,2048]{1,0:T(8,128)(2,1)S(1)} %shard_map.151.refs_1_), channel_id=1, source_target_pairs={{0,1},{1,0},{2,3},{3,2},{4,5},{5,4},{6,7},{7,6},{8,9},{9,8},{10,11... | collective-permute-start | bytes 196616 | tf_op jit(solution)/shard_map/ppermute | solution.py:24
  43.1 5.8 %collective-permute-start.14 = (bf16[16,512]{1,0:T(8,128)(2,1)S(1)}, bf16[16,512]{1,0:T(8,128)(2,1)S(1)}, u32[]{:S(2)}, u32[]{:S(2)}) collective-permute-start(bf16[16,512]{1,0:T(8,128)(2,1)S(1)} %shard_map.152.mine_ref), channel_id=1, source_target_pairs={{2,16},{6,20},{10,24},{14,28},{16,2},{20,6},{24,10},{28,14},{3,17}... | collective-permute-start | bytes 49160 | tf_op jit(solution)/shard_map/ppermute | solution.py:532
  43.8 6.6 %collective-permute-start.13 = (bf16[16,512]{1,0:T(8,128)(2,1)S(1)}, bf16[16,512]{1,0:T(8,128)(2,1)S(1)}, u32[]{:S(2)}, u32[]{:S(2)}) collective-permute-start(bf16[16,512]{1,0:T(8,128)(2,1)S(1)} %shard_map.152.mine_ref), channel_id=1, source_target_pairs={{2,0},{0,16},{6,4},{4,20},{10,8},{8,24},{14,12},{12,28},{16,18},{1... | collective-permute-start | bytes 49160 | tf_op jit(solution)/shard_map/ppermute | solution.py:531
  50.4 9.1 %slice-start = ((s8[7340032]{0:T(1024)(128)(4,1)}), s8[4194304]{0:T(1024)(128)(4,1)S(1)}, s32[]{:S(2)}) async-start(s8[7340032]{0:T(1024)(128)(4,1)} %bitcast.65), calls=%async_computation | async-start | bytes 8388608
  50.4 9.1 %slice-start.2 = ((s8[7340032]{0:T(1024)(128)(4,1)}), s8[4194304]{0:T(1024)(128)(4,1)S(1)}, s32[]{:S(2)}) async-start(s8[7340032]{0:T(1024)(128)(4,1)} %bitcast.67), calls=%async_computation.2 | async-start | bytes 8388608
  50.4 9.1 %slice-start.1 = ((s8[7340032]{0:T(1024)(128)(4,1)}), s8[3145728]{0:T(1024)(128)(4,1)S(1)}, s32[]{:S(2)}) async-start(s8[7340032]{0:T(1024)(128)(4,1)} %bitcast.65), calls=%async_computation.1 | async-start | bytes 6291456
  50.4 9.1 %slice-start.3 = ((s8[7340032]{0:T(1024)(128)(4,1)}), s8[3145728]{0:T(1024)(128)(4,1)S(1)}, s32[]{:S(2)}) async-start(s8[7340032]{0:T(1024)(128)(4,1)} %bitcast.67), calls=%async_computation.3 | async-start | bytes 6291456
  50.4 9.1 %copy-start.3 = (f32[8192]{0:T(1024)S(1)}, f32[8192]{0:T(1024)}, u32[]{:S(2)}) copy-start(f32[8192]{0:T(1024)} %param.19) | copy-start | bytes 98308
  50.4 3.8 %collective-permute-start.15 = (bf16[16,512]{1,0:T(8,128)(2,1)S(1)}, bf16[16,512]{1,0:T(8,128)(2,1)S(1)}, u32[]{:S(2)}, u32[]{:S(2)}) collective-permute-start(bf16[16,512]{1,0:T(8,128)(2,1)S(1)} %shard_map.153.one_ref), channel_id=1, source_target_pairs={{0,8},{4,12},{8,0},{12,4},{16,24},{20,28},{24,16},{28,20},{1,9},{5... | collective-permute-start | bytes 49160 | tf_op jit(solution)/shard_map/ppermute | solution.py:24
  54.2 3.9 %collective-permute-start.16 = (bf16[16,1024]{1,0:T(8,128)(2,1)S(1)}, bf16[16,1024]{1,0:T(8,128)(2,1)S(1)}, u32[]{:S(2)}, u32[]{:S(2)}) collective-permute-start(bf16[16,1024]{1,0:T(8,128)(2,1)S(1)} %shard_map.154.one_ref), channel_id=1, source_target_pairs={{0,4},{4,0},{8,12},{12,8},{16,20},{20,16},{24,28},{28,24},{1,5},{5... | collective-permute-start | bytes 98312 | tf_op jit(solution)/shard_map/ppermute | solution.py:24
  58.2 1.3 %collective-permute-start.17 = (bf16[16,2048]{1,0:T(8,128)(2,1)S(1)}, bf16[16,2048]{1,0:T(8,128)(2,1)S(1)}, u32[]{:S(2)}, u32[]{:S(2)}) collective-permute-start(bf16[16,2048]{1,0:T(8,128)(2,1)S(1)} %shard_map.155.one_ref), channel_id=1, source_target_pairs={{0,1},{1,0},{2,3},{3,2},{4,5},{5,4},{6,7},{7,6},{8,9},{9,8},{10,11... | collective-permute-start | bytes 196616 | tf_op jit(solution)/shard_map/ppermute | solution.py:24
  61.6 4.3 %collective-permute-start.18 = (bf16[16,1920]{1,0:T(8,128)(2,1)S(1)}, bf16[16,1920]{1,0:T(8,128)(2,1)S(1)}, u32[]{:S(2)}, u32[]{:S(2)}) collective-permute-start(bf16[16,1920]{1,0:T(8,128)(2,1)S(1)} %shard_map.158), channel_id=1, source_target_pairs={{0,2},{2,0},{1,3},{3,1},{4,6},{6,4},{5,7},{7,5},{8,10},{10,8},{9,1... | collective-permute-start | bytes 184328 | tf_op jit(solution)/shard_map/ppermute | solution.py:24
  67.2 1.3 %collective-permute-start.19 = (bf16[8,4096]{1,0:T(8,128)(2,1)S(1)}, bf16[8,4096]{1,0:T(8,128)(2,1)S(1)}, u32[]{:S(2)}, u32[]{:S(2)}) collective-permute-start(bf16[8,4096]{1,0:T(8,128)(2,1)S(1)} %get-tuple-element.42), channel_id=1, source_target_pairs={{0,1},{1,0},{2,3},{3,2},{4,5},{5,4},{6,7},{7,6},{8,9},{9,8},{10,11... | collective-permute-start | bytes 196616 | tf_op jit(solution)/shard_map/ppermute | solution.py:24
  68.5 4.0 %collective-permute-start.20 = (bf16[4,4096]{1,0:T(4,128)(2,1)S(1)}, bf16[4,4096]{1,0:T(4,128)(2,1)S(1)}, u32[]{:S(2)}, u32[]{:S(2)}) collective-permute-start(bf16[4,4096]{1,0:T(4,128)(2,1)S(1)} %select_convert_fusion), channel_id=1, source_target_pairs={{0,4},{4,0},{8,12},{12,8},{16,20},{20,16},{24,28},{28,24},{1,5},{5... | collective-permute-start | bytes 98312 | tf_op jit(solution)/shard_map/ppermute | solution.py:24
  72.7 4.7 %collective-permute-start.21 = (bf16[1,4096]{1,0:T(2,128)(2,1)S(1)}, bf16[1,4096]{1,0:T(2,128)(2,1)S(1)}, u32[]{:S(2)}, u32[]{:S(2)}) collective-permute-start(bf16[1,4096]{1,0:T(2,128)(2,1)S(1)} %get-tuple-element.50), channel_id=1, source_target_pairs={{0,8},{4,12},{8,0},{12,4},{16,24},{20,28},{24,16},{28,20},{1,9},{5... | collective-permute-start | bytes 24584 | tf_op jit(solution)/shard_map/ppermute | solution.py:24
  74.7 5.5 %collective-permute-start.23 = (bf16[1,4096]{1,0:T(2,128)(2,1)S(1)}, bf16[1,4096]{1,0:T(2,128)(2,1)S(1)}, u32[]{:S(2)}, u32[]{:S(2)}) collective-permute-start(bf16[1,4096]{1,0:T(2,128)(2,1)S(1)} %get-tuple-element.51), channel_id=1, source_target_pairs={{0,24},{4,28},{8,16},{12,20},{16,8},{20,12},{24,0},{28,4},{1,25},{... | collective-permute-start | bytes 24584 | tf_op jit(solution)/shard_map/ppermute | solution.py:24
  77.4 4.6 %collective-permute-start.22 = (bf16[1,4096]{1,0:T(2,128)(2,1)S(1)}, bf16[1,4096]{1,0:T(2,128)(2,1)S(1)}, u32[]{:S(2)}, u32[]{:S(2)}) collective-permute-start(bf16[1,4096]{1,0:T(2,128)(2,1)S(1)} %get-tuple-element.52), channel_id=1, source_target_pairs={{0,16},{4,20},{8,24},{12,28},{16,0},{20,4},{24,8},{28,12},{1,17},{... | collective-permute-start | bytes 24584 | tf_op jit(solution)/shard_map/ppermute | solution.py:24
  (6 other events, 24.1 us)
where the time goes:
time: 82.9 us; the launch traced here: 82.7 us
  waiting for transfers between devices  37.8 us (46%)
  starting transfers between devices  32.7 us (39%)
  Pallas kernels  5.91 us (7%)
  other arithmetic  2.37 us (3%)
  matrix products  2.31 us (3%)
  local copies, waits for them, and re-layouts  1.25 us (2%)
    ppermute x22, waiting for transfers between devices, swap(): return lax.ppermute(x, axis, [(i, i ^ bit) for i in range(size)])  36.3 us
    ppermute x22, starting transfers between devices, swap(): return lax.ppermute(x, axis, [(i, i ^ bit) for i in range(size)])  26.8 us
    ppermute x1, starting transfers between devices, shards(): got = lax.ppermute(middle, ('seq', 'head'), near)  5.15 us
    pallas_call x4, Pallas kernels, weight_call(): pl.pallas_call(kernel, out_shape=outs, in_specs=[pl.BlockSpec(memory_spac...  4.59 us
  transfers between devices with their start and end apart: 24, of which 20 were waited for; matrix products, arithmetic and copies ran while one was open for 2% of the time, Pallas kernels for 0%

commit v1 on v0

--- a/solution.py
+++ b/solution.py
@@ -297,13 +297,15 @@
         out_ref[rows, :] = (total[rows] + own).astype(BF16)
 
 
-def wide_kernel(local, places, weights, x_ref, gain_ref, *outs):
-    gate, up, tail_ref, own_ref = outs
+def wide_kernel(local, places, weights, x_ref, gain_ref, *refs):
+    gate, up, tail_ref, own_ref = refs[-4:]
+    before = refs[:-4]
     wide = x_ref.shape[1]
     x = x_ref[...].astype(F32)
     squares = jnp.sum(x * x, axis=1, keepdims=True)
     lane = lax.broadcasted_iota(jnp.int32, tail_ref.shape, 1)
     tail_ref[...] = jnp.where(lane == 0, squares, 0.0)
+    own_ref[...] = before[3][...] if before else jnp.zeros(own_ref.shape, F32)
     sums = [None] * len(weights)
     row = lax.broadcasted_iota(jnp.int32, (x.shape[0], local), 0)
     for b in range(wide // local):
@@ -319,17 +321,19 @@
         for n, weight in enumerate(weights):
             got = jnp.dot(part, weight[pl.ds(start, local), :], preferred_element_type=F32)
             sums[n] = got if sums[n] is None else sums[n] + got
-    gate[...] = sums[0]
-    up[...] = sums[1]
-
-
-def wide_call(weights, places, local, share, x, gain):
+    gate[...] = sums[0] + before[0][...] if before else sums[0]
+    up[...] = sums[1] + before[1][...] if before else sums[1]
+    if before:
+        tail_ref[...] += before[2][...]
+
+
+def wide_call(weights, places, local, share, x, gain, before=()):
     rows = x.shape[0]
     outs = [jax.ShapeDtypeStruct((rows, weights[0].shape[1]), F32)] * 2
     outs.append(jax.ShapeDtypeStruct((rows, 128), F32))
-    outs.append(jax.ShapeDtypeStruct((share, x.shape[1]), F32))
+    outs.append(jax.ShapeDtypeStruct((share, weights[0].shape[0]), F32))
     body = functools.partial(wide_kernel, local, places)
-    return weight_call(body, tuple(outs), weights, x, gain)
+    return weight_call(body, tuple(outs), weights, x, gain, *before)
 
 
 def pack_kernel(gate_ref, up_ref, tail_ref, out_ref):
@@ -533,13 +537,18 @@
         middle = arrive(lanes // 2, middle, got, away)
         stages = [("seq", bit) for bit in sorted(bits_of(half), reverse=True)] + [("rep", 1)]
         turns = [0]
-        for axis, bit in stages:
+        for axis, bit in stages[:-1]:
             middle = join(middle, swap(middle, axis, bit))
-            turns += [turn ^ (1 if axis == "rep" else 2 * bit) for turn in turns]
-
-        def places(b):
-            return (lane_index() % (lanes // 2)) ^ turns[b]
-
+            turns += [turn ^ (2 * bit) for turn in turns]
+
+        def places(turn, b):
+            return (lane_index() % (lanes // 2)) ^ turns[b] ^ turn
+
+        mine = functools.partial(places, 0)
+        middle, rest = lax.optimization_barrier(
+            (swap(middle, "rep", 1), wide_call(weights, mine, local, share, middle, gain))
+        )
+        places = functools.partial(places, 1)
     else:
         for bit in bits_of(groups):
             middle = (middle.astype(F32) + swap(middle, "head", bit).astype(F32)).astype(BF16)
@@ -549,7 +558,11 @@
         def places(b):
             return b
 
-    gate, up, tail, own_middle = wide_call(weights, places, local, share, middle, gain)
+        rest = ()
+
+    gate, up, tail, own_middle = wide_call(
+        weights, places, local, share, middle, gain, rest
+    )
 
     ff_local = w_gate.shape[1]
     for bit in bits_of(groups):

time: 82.9 us -> 82.2 us (level)
  waiting for transfers between devices: 37.8 us -> 36.9 us
    ppermute x22, waiting for transfers between devices: 36.3 us -> 35.5 us  [swap(): return lax.ppermute(x, axis, [(i, i ^ bit) for i in range(size)])]
    pallas_call x4 -> x5, Pallas kernels: 4.59 us -> 4.71 us  [weight_call(): pl.pallas_call(kernel, out_shape=outs, in_specs=[pl.BlockSpec(memory_spac...]
  transfers between devices with their start and end apart: 24 -> 24, of which waited for: 20 -> 20; matrix products, arithmetic and copies ran while one was open for 2% -> 2% of each run, Pallas kernels for 0% -> 1%
where the time goes in v1:
time: 82.2 us; the launch traced here: 82 us
  waiting for transfers between devices  36.9 us (45%)
  starting transfers between devices  32.7 us (40%)
  Pallas kernels  6.02 us (7%)
  other arithmetic  2.37 us (3%)
  matrix products  2.31 us (3%)
  local copies, waits for them, and re-layouts  1.25 us (2%)
    ppermute x22, waiting for transfers between devices, swap(): return lax.ppermute(x, axis, [(i, i ^ bit) for i in range(size)])  35.5 us
    ppermute x22, starting transfers between devices, swap(): return lax.ppermute(x, axis, [(i, i ^ bit) for i in range(size)])  26.6 us
    ppermute x1, starting transfers between devices, shards(): got = lax.ppermute(middle, ('seq', 'head'), near)  5.29 us
    pallas_call x5, Pallas kernels, weight_call(): pl.pallas_call(kernel, out_shape=outs, in_specs=[pl.BlockSpec(memory_spac...  4.71 us
  transfers between devices with their start and end apart: 24, of which 20 were waited for; matrix products, arithmetic and copies ran while one was open for 2% of the time, Pallas kernels for 1%

profile of v1, /device:TPU:0, one launch (start us, length us, event | category | flops | bytes accessed | tf_op | source)
XLA Modules:
  0.0 82.0 jit_solution(160448789288884701)
XLA Ops:
  0.0 1.1 %multiply_reduce_fusion = (f32[8]{0:T(128)S(1)}, bf16[8,512]{1,0:T(8,128)(2,1)S(1)}, f32[8,512]{1,0:T(8,128)S(1)}) fusion(f32[512]{0:T(512)} %param.18, f32[8,16]{1,0:T(8,128)} %param.16, f32[16,512]{1,0:T(8,128)} %param.17, bf16[8,512]{1,0:T(8,128)(2,1)} %param.15), kind=kOutput, calls=%fused_computation.42 | convolution fusion | flops 811000 | bytes 68128 | tf_op jit(solution)/shard_map/dot_general | solution.py:417
  1.3 3.0 %collective-permute-start = (bf16[8,640]{1,0:T(8,128)(2,1)S(1)}, bf16[8,640]{1,0:T(8,128)(2,1)S(1)}, u32[]{:S(2)}, u32[]{:S(2)}) collective-permute-start(bf16[8,640]{1,0:T(8,128)(2,1)S(1)} %shard_map.145.refs_1_), channel_id=1, source_target_pairs={{0,2},{2,0},{1,3},{3,1},{4,6},{6,4},{5,7},{7,5},{8,10},{10,8},{9,1... | collective-permute-start | bytes 30728 | tf_op jit(solution)/shard_map/ppermute | solution.py:24
  4.2 1.6 %collective-permute-done.refs_2_ = bf16[8,640]{1,0:T(8,128)(2,1)S(1)} collective-permute-done((bf16[8,640]{1,0:T(8,128)(2,1)S(1)}, bf16[8,640]{1,0:T(8,128)(2,1)S(1)}, u32[]{:S(2)}, u32[]{:S(2)}) %collective-permute-start) | collective-permute-done | bytes 10272 | tf_op jit(solution)/shard_map/ppermute | solution.py:24
  6.6 1.2 %collective-permute-done.1 = bf16[16,2176]{1,0:T(8,128)(2,1)S(1)} collective-permute-done((bf16[16,2176]{1,0:T(8,128)(2,1)S(1)}, bf16[16,2176]{1,0:T(8,128)(2,1)S(1)}, u32[]{:S(2)}, u32[]{:S(2)}) %collective-permute-start.1) | collective-permute-done | bytes 69664 | tf_op jit(solution)/shard_map/ppermute | solution.py:24
  7.8 2.1 %collective-permute-start.2 = (bf16[16,2176]{1,0:T(8,128)(2,1)S(1)}, bf16[16,2176]{1,0:T(8,128)(2,1)S(1)}, u32[]{:S(2)}, u32[]{:S(2)}) collective-permute-start(bf16[16,2176]{1,0:T(8,128)(2,1)S(1)} %get-tuple-element.64), channel_id=1, source_target_pairs={{0,4},{4,0},{8,12},{12,8},{16,20},{20,16},{24,28},{28,24},{1,5},{5... | collective-permute-start | bytes 208904 | tf_op jit(solution)/shard_map/ppermute | solution.py:24
  10.7 1.8 %collective-permute-done.2.refs_0_ = bf16[16,2176]{1,0:T(8,128)(2,1)S(1)} collective-permute-done((bf16[16,2176]{1,0:T(8,128)(2,1)S(1)}, bf16[16,2176]{1,0:T(8,128)(2,1)S(1)}, u32[]{:S(2)}, u32[]{:S(2)}) %collective-permute-start.2) | collective-permute-done | bytes 69664 | tf_op jit(solution)/shard_map/ppermute | solution.py:24
  12.5 4.0 %collective-permute-start.5 = (bf16[16,2176]{1,0:T(8,128)(2,1)S(1)}, bf16[16,2176]{1,0:T(8,128)(2,1)S(1)}, u32[]{:S(2)}, u32[]{:S(2)}) collective-permute-start(bf16[16,2176]{1,0:T(8,128)(2,1)S(1)} %get-tuple-element.36), channel_id=1, source_target_pairs={{0,24},{4,28},{8,16},{12,20},{16,8},{20,12},{24,0},{28,4},{1,25},{... | collective-permute-start | bytes 208904 | tf_op jit(solution)/shard_map/ppermute | solution.py:24
  17.2 2.1 %collective-permute-done.5.refs_2_ = bf16[16,2176]{1,0:T(8,128)(2,1)S(1)} collective-permute-done((bf16[16,2176]{1,0:T(8,128)(2,1)S(1)}, bf16[16,2176]{1,0:T(8,128)(2,1)S(1)}, u32[]{:S(2)}, u32[]{:S(2)}) %collective-permute-start.5) | collective-permute-done | bytes 69664 | tf_op jit(solution)/shard_map/ppermute | solution.py:24
  19.3 2.6 %collective-permute-done.4.refs_1_ = bf16[16,2176]{1,0:T(8,128)(2,1)S(1)} collective-permute-done((bf16[16,2176]{1,0:T(8,128)(2,1)S(1)}, bf16[16,2176]{1,0:T(8,128)(2,1)S(1)}, u32[]{:S(2)}, u32[]{:S(2)}) %collective-permute-start.4) | collective-permute-done | bytes 69664 | tf_op jit(solution)/shard_map/ppermute | solution.py:24
  27.5 1.6 %collective-permute-start.8 = (bf16[16,2176]{1,0:T(8,128)(2,1)S(1)}, bf16[16,2176]{1,0:T(8,128)(2,1)S(1)}, u32[]{:S(2)}, u32[]{:S(2)}) collective-permute-start(bf16[16,2176]{1,0:T(8,128)(2,1)S(1)} %get-tuple-element.39), channel_id=1, source_target_pairs={{0,4},{4,0},{8,12},{12,8},{16,20},{20,16},{24,28},{28,24},{1,5},{5... | collective-permute-start | bytes 208904 | tf_op jit(solution)/shard_map/ppermute | solution.py:24
  29.1 2.8 %collective-permute-done.8.refs_0_ = bf16[16,2176]{1,0:T(8,128)(2,1)S(1)} collective-permute-done((bf16[16,2176]{1,0:T(8,128)(2,1)S(1)}, bf16[16,2176]{1,0:T(8,128)(2,1)S(1)}, u32[]{:S(2)}, u32[]{:S(2)}) %collective-permute-start.8) | collective-permute-done | bytes 69664 | tf_op jit(solution)/shard_map/ppermute | solution.py:24
  32.1 2.6 %collective-permute-start.11 = (bf16[16,2176]{1,0:T(8,128)(2,1)S(1)}, bf16[16,2176]{1,0:T(8,128)(2,1)S(1)}, u32[]{:S(2)}, u32[]{:S(2)}) collective-permute-start(bf16[16,2176]{1,0:T(8,128)(2,1)S(1)} %get-tuple-element.42), channel_id=1, source_target_pairs={{0,24},{4,28},{8,16},{12,20},{16,8},{20,12},{24,0},{28,4},{1,25},{... | collective-permute-start | bytes 208904 | tf_op jit(solution)/shard_map/ppermute | solution.py:24
  34.7 1.9 %collective-permute-start.9 = (bf16[16,2176]{1,0:T(8,128)(2,1)S(1)}, bf16[16,2176]{1,0:T(8,128)(2,1)S(1)}, u32[]{:S(2)}, u32[]{:S(2)}) collective-permute-start(bf16[16,2176]{1,0:T(8,128)(2,1)S(1)} %get-tuple-element.42), channel_id=1, source_target_pairs={{0,8},{4,12},{8,0},{12,4},{16,24},{20,28},{24,16},{28,20},{1,9},{5... | collective-permute-start | bytes 208904 | tf_op jit(solution)/shard_map/ppermute | solution.py:24
  36.6 2.0 %collective-permute-done.11.refs_2_ = bf16[16,2176]{1,0:T(8,128)(2,1)S(1)} collective-permute-done((bf16[16,2176]{1,0:T(8,128)(2,1)S(1)}, bf16[16,2176]{1,0:T(8,128)(2,1)S(1)}, u32[]{:S(2)}, u32[]{:S(2)}) %collective-permute-start.11) | collective-permute-done | bytes 69664 | tf_op jit(solution)/shard_map/ppermute | solution.py:24
  38.5 2.3 %collective-permute-done.10.refs_1_ = bf16[16,2176]{1,0:T(8,128)(2,1)S(1)} collective-permute-done((bf16[16,2176]{1,0:T(8,128)(2,1)S(1)}, bf16[16,2176]{1,0:T(8,128)(2,1)S(1)}, u32[]{:S(2)}, u32[]{:S(2)}) %collective-permute-start.10) | collective-permute-done | bytes 69664 | tf_op jit(solution)/shard_map/ppermute | solution.py:24
  41.2 1.2 %collective-permute-done.12.refs_2_ = bf16[16,2048]{1,0:T(8,128)(2,1)S(1)} collective-permute-done((bf16[16,2048]{1,0:T(8,128)(2,1)S(1)}, bf16[16,2048]{1,0:T(8,128)(2,1)S(1)}, u32[]{:S(2)}, u32[]{:S(2)}) %collective-permute-start.12) | collective-permute-done | bytes 65568 | tf_op jit(solution)/shard_map/ppermute | solution.py:24
  43.9 5.3 %collective-permute-start.13 = (bf16[16,512]{1,0:T(8,128)(2,1)S(1)}, bf16[16,512]{1,0:T(8,128)(2,1)S(1)}, u32[]{:S(2)}, u32[]{:S(2)}) collective-permute-start(bf16[16,512]{1,0:T(8,128)(2,1)S(1)} %shard_map.152.mine_ref), channel_id=1, source_target_pairs={{2,0},{0,16},{6,4},{4,20},{10,8},{8,24},{14,12},{12,28},{16,18},{1... | collective-permute-start | bytes 49160 | tf_op jit(solution)/shard_map/ppermute | solution.py:535
  49.2 1.4 %collective-permute-done.13.near_ref = bf16[16,512]{1,0:T(8,128)(2,1)S(1)} collective-permute-done((bf16[16,512]{1,0:T(8,128)(2,1)S(1)}, bf16[16,512]{1,0:T(8,128)(2,1)S(1)}, u32[]{:S(2)}, u32[]{:S(2)}) %collective-permute-start.13) | collective-permute-done | bytes 16416 | tf_op jit(solution)/shard_map/ppermute | solution.py:535
  51.7 2.8 %collective-permute-done.15.two_ref = bf16[16,512]{1,0:T(8,128)(2,1)S(1)} collective-permute-done((bf16[16,512]{1,0:T(8,128)(2,1)S(1)}, bf16[16,512]{1,0:T(8,128)(2,1)S(1)}, u32[]{:S(2)}, u32[]{:S(2)}) %collective-permute-start.15) | collective-permute-done | bytes 16416 | tf_op jit(solution)/shard_map/ppermute | solution.py:24
  54.5 1.5 %collective-permute-start.16 = (bf16[16,1024]{1,0:T(8,128)(2,1)S(1)}, bf16[16,1024]{1,0:T(8,128)(2,1)S(1)}, u32[]{:S(2)}, u32[]{:S(2)}) collective-permute-start(bf16[16,1024]{1,0:T(8,128)(2,1)S(1)} %shard_map.154.one_ref), channel_id=1, source_target_pairs={{0,4},{4,0},{8,12},{12,8},{16,20},{20,16},{24,28},{28,24},{1,5},{5... | collective-permute-start | bytes 98312 | tf_op jit(solution)/shard_map/ppermute | solution.py:24
  56.0 2.4 %collective-permute-done.16.two_ref = bf16[16,1024]{1,0:T(8,128)(2,1)S(1)} collective-permute-done((bf16[16,1024]{1,0:T(8,128)(2,1)S(1)}, bf16[16,1024]{1,0:T(8,128)(2,1)S(1)}, u32[]{:S(2)}, u32[]{:S(2)}) %collective-permute-start.16) | collective-permute-done | bytes 32800 | tf_op jit(solution)/shard_map/ppermute | solution.py:24
  58.5 1.1 %shard_map.156 = (f32[16,896]{1,0:T(8,128)S(1)}, f32[16,896]{1,0:T(8,128)S(1)}, f32[16,128]{1,0:T(8,128)S(1)}, f32[1,4096]{1,0:T(1,128)S(1)}) custom-call(bf16[4096,896]{1,0:T(8,128)(2,1)S(1)} %bitcast.66, bf16[4096,896]{1,0:T(8,128)(2,1)S(1)} %bitcast.68, bf16[16,2048]{1,0:T(8,128)(2,1)S(1)} %shard_map.155.refs_2_, f32[1,8192]{1,0:T(1,128)S(1)} %bitcast.71), custom_call_target="tpu_custom_call" | custom-call | bytes 14680064 | tf_op jit(solution)/shard_map/pallas_call | solution.py:238
  60.8 2.1 %collective-permute-start.18 = (bf16[16,1920]{1,0:T(8,128)(2,1)S(1)}, bf16[16,1920]{1,0:T(8,128)(2,1)S(1)}, u32[]{:S(2)}, u32[]{:S(2)}) collective-permute-start(bf16[16,1920]{1,0:T(8,128)(2,1)S(1)} %shard_map.158), channel_id=1, source_target_pairs={{0,2},{2,0},{1,3},{3,1},{4,6},{6,4},{5,7},{7,5},{8,10},{10,8},{9,1... | collective-permute-start | bytes 184328 | tf_op jit(solution)/shard_map/ppermute | solution.py:24
  62.9 2.6 %collective-permute-done.18.got_ref = bf16[16,1920]{1,0:T(8,128)(2,1)S(1)} collective-permute-done((bf16[16,1920]{1,0:T(8,128)(2,1)S(1)}, bf16[16,1920]{1,0:T(8,128)(2,1)S(1)}, u32[]{:S(2)}, u32[]{:S(2)}) %collective-permute-start.18) | collective-permute-done | bytes 61472 | tf_op jit(solution)/shard_map/ppermute | solution.py:24
  65.5 1.2 %shard_map.160 = (f32[8,4096]{1,0:T(8,128)S(1)}, bf16[8,4096]{1,0:T(8,128)(2,1)S(1)}) custom-call(bf16[896,4096]{1,0:T(8,128)(2,1)S(1)} %bitcast.70, f32[16,896]{1,0:T(8,128)S(1)} %get-tuple-element.56.refs_1_, f32[16,896]{1,0:T(8,128)S(1)} %get-tuple-element.57.refs_2_, f32[16,128]{1,0:T(8,128)S(1)} %get-tuple-element.58.refs_3_), custom_call_target="tpu_custom_call" | custom-call | bytes 7340032 | tf_op jit(solution)/shard_map/pallas_call | solution.py:238
  66.8 1.3 %collective-permute-done.19 = bf16[8,4096]{1,0:T(8,128)(2,1)S(1)} collective-permute-done((bf16[8,4096]{1,0:T(8,128)(2,1)S(1)}, bf16[8,4096]{1,0:T(8,128)(2,1)S(1)}, u32[]{:S(2)}, u32[]{:S(2)}) %collective-permute-start.19) | collective-permute-done | bytes 65568 | tf_op jit(solution)/shard_map/ppermute | solution.py:24
  68.1 1.5 %collective-permute-start.20 = (bf16[4,4096]{1,0:T(4,128)(2,1)S(1)}, bf16[4,4096]{1,0:T(4,128)(2,1)S(1)}, u32[]{:S(2)}, u32[]{:S(2)}) collective-permute-start(bf16[4,4096]{1,0:T(4,128)(2,1)S(1)} %select_convert_fusion), channel_id=1, source_target_pairs={{0,4},{4,0},{8,12},{12,8},{16,20},{20,16},{24,28},{28,24},{1,5},{5... | collective-permute-start | bytes 98312 | tf_op jit(solution)/shard_map/ppermute | solution.py:24
  69.6 2.5 %collective-permute-done.20 = bf16[4,4096]{1,0:T(4,128)(2,1)S(1)} collective-permute-done((bf16[4,4096]{1,0:T(4,128)(2,1)S(1)}, bf16[4,4096]{1,0:T(4,128)(2,1)S(1)}, u32[]{:S(2)}, u32[]{:S(2)}) %collective-permute-start.20) | collective-permute-done | bytes 32800 | tf_op jit(solution)/shard_map/ppermute | solution.py:24
  72.3 1.9 %collective-permute-start.21 = (bf16[1,4096]{1,0:T(2,128)(2,1)S(1)}, bf16[1,4096]{1,0:T(2,128)(2,1)S(1)}, u32[]{:S(2)}, u32[]{:S(2)}) collective-permute-start(bf16[1,4096]{1,0:T(2,128)(2,1)S(1)} %get-tuple-element.68), channel_id=1, source_target_pairs={{0,8},{4,12},{8,0},{12,4},{16,24},{20,28},{24,16},{28,20},{1,9},{5... | collective-permute-start | bytes 24584 | tf_op jit(solution)/shard_map/ppermute | solution.py:24
  74.1 2.5 %collective-permute-start.23 = (bf16[1,4096]{1,0:T(2,128)(2,1)S(1)}, bf16[1,4096]{1,0:T(2,128)(2,1)S(1)}, u32[]{:S(2)}, u32[]{:S(2)}) collective-permute-start(bf16[1,4096]{1,0:T(2,128)(2,1)S(1)} %get-tuple-element.69), channel_id=1, source_target_pairs={{0,24},{4,28},{8,16},{12,20},{16,8},{20,12},{24,0},{28,4},{1,25},{... | collective-permute-start | bytes 24584 | tf_op jit(solution)/shard_map/ppermute | solution.py:24
  76.7 3.0 %collective-permute-done.23 = bf16[1,4096]{1,0:T(2,128)(2,1)S(1)} collective-permute-done((bf16[1,4096]{1,0:T(2,128)(2,1)S(1)}, bf16[1,4096]{1,0:T(2,128)(2,1)S(1)}, u32[]{:S(2)}, u32[]{:S(2)}) %collective-permute-start.23) | collective-permute-done | bytes 8224 | tf_op jit(solution)/shard_map/ppermute | solution.py:24
  79.7 1.6 %collective-permute-done.22 = bf16[1,4096]{1,0:T(2,128)(2,1)S(1)} collective-permute-done((bf16[1,4096]{1,0:T(2,128)(2,1)S(1)}, bf16[1,4096]{1,0:T(2,128)(2,1)S(1)}, u32[]{:S(2)}, u32[]{:S(2)}) %collective-permute-start.22) | collective-permute-done | bytes 8224 | tf_op jit(solution)/shard_map/ppermute | solution.py:24
  (104 shorter events, 13.1 us)
Async XLA Ops:
  0.0 24.0 %copy-start = (bf16[512,4,128]{2,1,0:T(4,128)(2,1)S(1)}, bf16[512,4,128]{2,1,0:T(4,128)(2,1)}, u32[]{:S(2)}) copy-start(bf16[512,4,128]{2,1,0:T(4,128)(2,1)} %param.25) | copy-start | bytes 1572868
  1.3 4.6 %collective-permute-start = (bf16[8,640]{1,0:T(8,128)(2,1)S(1)}, bf16[8,640]{1,0:T(8,128)(2,1)S(1)}, u32[]{:S(2)}, u32[]{:S(2)}) collective-permute-start(bf16[8,640]{1,0:T(8,128)(2,1)S(1)} %shard_map.145.refs_1_), channel_id=1, source_target_pairs={{0,2},{2,0},{1,3},{3,1},{4,6},{6,4},{5,7},{7,5},{8,10},{10,8},{9,1... | collective-permute-start | bytes 30728 | tf_op jit(solution)/shard_map/ppermute | solution.py:24
  6.5 1.3 %collective-permute-start.1 = (bf16[16,2176]{1,0:T(8,128)(2,1)S(1)}, bf16[16,2176]{1,0:T(8,128)(2,1)S(1)}, u32[]{:S(2)}, u32[]{:S(2)}) collective-permute-start(bf16[16,2176]{1,0:T(8,128)(2,1)S(1)} %get-tuple-element.34), channel_id=1, source_target_pairs={{0,1},{1,0},{2,3},{3,2},{4,5},{5,4},{6,7},{7,6},{8,9},{9,8},{10,11... | collective-permute-start | bytes 208904 | tf_op jit(solution)/shard_map/ppermute | solution.py:24
  7.8 4.6 %collective-permute-start.2 = (bf16[16,2176]{1,0:T(8,128)(2,1)S(1)}, bf16[16,2176]{1,0:T(8,128)(2,1)S(1)}, u32[]{:S(2)}, u32[]{:S(2)}) collective-permute-start(bf16[16,2176]{1,0:T(8,128)(2,1)S(1)} %get-tuple-element.64), channel_id=1, source_target_pairs={{0,4},{4,0},{8,12},{12,8},{16,20},{20,16},{24,28},{28,24},{1,5},{5... | collective-permute-start | bytes 208904 | tf_op jit(solution)/shard_map/ppermute | solution.py:24
  12.5 11.0 %copy-start.4 = (bf16[1,128,4,128]{3,2,1,0:T(4,128)(2,1)S(1)}, bf16[1,128,4,128]{3,2,1,0:T(4,128)(2,1)}, u32[]{:S(2)}) copy-start(bf16[1,128,4,128]{3,2,1,0:T(4,128)(2,1)} %param.27) | copy-start | bytes 393220
  12.5 6.8 %collective-permute-start.5 = (bf16[16,2176]{1,0:T(8,128)(2,1)S(1)}, bf16[16,2176]{1,0:T(8,128)(2,1)S(1)}, u32[]{:S(2)}, u32[]{:S(2)}) collective-permute-start(bf16[16,2176]{1,0:T(8,128)(2,1)S(1)} %get-tuple-element.36), channel_id=1, source_target_pairs={{0,24},{4,28},{8,16},{12,20},{16,8},{20,12},{24,0},{28,4},{1,25},{... | collective-permute-start | bytes 208904 | tf_op jit(solution)/shard_map/ppermute | solution.py:24
  16.4 5.5 %collective-permute-start.4 = (bf16[16,2176]{1,0:T(8,128)(2,1)S(1)}, bf16[16,2176]{1,0:T(8,128)(2,1)S(1)}, u32[]{:S(2)}, u32[]{:S(2)}) collective-permute-start(bf16[16,2176]{1,0:T(8,128)(2,1)S(1)} %get-tuple-element.36), channel_id=1, source_target_pairs={{0,16},{4,20},{8,24},{12,28},{16,0},{20,4},{24,8},{28,12},{1,17},{... | collective-permute-start | bytes 208904 | tf_op jit(solution)/shard_map/ppermute | solution.py:24
  16.5 5.5 %collective-permute-start.3 = (bf16[16,2176]{1,0:T(8,128)(2,1)S(1)}, bf16[16,2176]{1,0:T(8,128)(2,1)S(1)}, u32[]{:S(2)}, u32[]{:S(2)}) collective-permute-start(bf16[16,2176]{1,0:T(8,128)(2,1)S(1)} %get-tuple-element.36), channel_id=1, source_target_pairs={{0,8},{4,12},{8,0},{12,4},{16,24},{20,28},{24,16},{28,20},{1,9},{5... | collective-permute-start | bytes 208904 | tf_op jit(solution)/shard_map/ppermute | solution.py:24
  22.1 1.3 %collective-permute-start.6 = (bf16[16,2048]{1,0:T(8,128)(2,1)S(1)}, bf16[16,2048]{1,0:T(8,128)(2,1)S(1)}, u32[]{:S(2)}, u32[]{:S(2)}) collective-permute-start(bf16[16,2048]{1,0:T(8,128)(2,1)S(1)} %shard_map.148), channel_id=1, source_target_pairs={{0,1},{1,0},{2,3},{3,2},{4,5},{5,4},{6,7},{7,6},{8,9},{9,8},{10,11... | collective-permute-start | bytes 196616 | tf_op jit(solution)/shard_map/ppermute | solution.py:24
  25.9 1.3 %collective-permute-start.7 = (bf16[16,2176]{1,0:T(8,128)(2,1)S(1)}, bf16[16,2176]{1,0:T(8,128)(2,1)S(1)}, u32[]{:S(2)}, u32[]{:S(2)}) collective-permute-start(bf16[16,2176]{1,0:T(8,128)(2,1)S(1)} %pad_maximum_fusion), channel_id=1, source_target_pairs={{0,1},{1,0},{2,3},{3,2},{4,5},{5,4},{6,7},{7,6},{8,9},{9,8},{10,11... | collective-permute-start | bytes 208904 | tf_op jit(solution)/shard_map/ppermute | solution.py:24
  27.5 4.4 %collective-permute-start.8 = (bf16[16,2176]{1,0:T(8,128)(2,1)S(1)}, bf16[16,2176]{1,0:T(8,128)(2,1)S(1)}, u32[]{:S(2)}, u32[]{:S(2)}) collective-permute-start(bf16[16,2176]{1,0:T(8,128)(2,1)S(1)} %get-tuple-element.39), channel_id=1, source_target_pairs={{0,4},{4,0},{8,12},{12,8},{16,20},{20,16},{24,28},{28,24},{1,5},{5... | collective-permute-start | bytes 208904 | tf_op jit(solution)/shard_map/ppermute | solution.py:24
  32.1 10.4 %copy-start.2 = (bf16[4096,512]{1,0:T(8,128)(2,1)S(1)}, bf16[4096,512]{1,0:T(8,128)(2,1)}, u32[]{:S(2)}) copy-start(bf16[4096,512]{1,0:T(8,128)(2,1)} %refs_0_.6) | copy-start | bytes 12582916
  32.1 6.4 %collective-permute-start.11 = (bf16[16,2176]{1,0:T(8,128)(2,1)S(1)}, bf16[16,2176]{1,0:T(8,128)(2,1)S(1)}, u32[]{:S(2)}, u32[]{:S(2)}) collective-permute-start(bf16[16,2176]{1,0:T(8,128)(2,1)S(1)} %get-tuple-element.42), channel_id=1, source_target_pairs={{0,24},{4,28},{8,16},{12,20},{16,8},{20,12},{24,0},{28,4},{1,25},{... | collective-permute-start | bytes 208904 | tf_op jit(solution)/shard_map/ppermute | solution.py:24
  34.7 6.1 %collective-permute-start.10 = (bf16[16,2176]{1,0:T(8,128)(2,1)S(1)}, bf16[16,2176]{1,0:T(8,128)(2,1)S(1)}, u32[]{:S(2)}, u32[]{:S(2)}) collective-permute-start(bf16[16,2176]{1,0:T(8,128)(2,1)S(1)} %get-tuple-element.42), channel_id=1, source_target_pairs={{0,16},{4,20},{8,24},{12,28},{16,0},{20,4},{24,8},{28,12},{1,17},{... | collective-permute-start | bytes 208904 | tf_op jit(solution)/shard_map/ppermute | solution.py:24
  34.7 6.1 %collective-permute-start.9 = (bf16[16,2176]{1,0:T(8,128)(2,1)S(1)}, bf16[16,2176]{1,0:T(8,128)(2,1)S(1)}, u32[]{:S(2)}, u32[]{:S(2)}) collective-permute-start(bf16[16,2176]{1,0:T(8,128)(2,1)S(1)} %get-tuple-element.42), channel_id=1, source_target_pairs={{0,8},{4,12},{8,0},{12,4},{16,24},{20,28},{24,16},{28,20},{1,9},{5... | collective-permute-start | bytes 208904 | tf_op jit(solution)/shard_map/ppermute | solution.py:24
  41.1 1.3 %collective-permute-start.12 = (bf16[16,2048]{1,0:T(8,128)(2,1)S(1)}, bf16[16,2048]{1,0:T(8,128)(2,1)S(1)}, u32[]{:S(2)}, u32[]{:S(2)}) collective-permute-start(bf16[16,2048]{1,0:T(8,128)(2,1)S(1)} %shard_map.151.refs_1_), channel_id=1, source_target_pairs={{0,1},{1,0},{2,3},{3,2},{4,5},{5,4},{6,7},{7,6},{8,9},{9,8},{10,11... | collective-permute-start | bytes 196616 | tf_op jit(solution)/shard_map/ppermute | solution.py:24
  42.5 16.0 %slice-start = ((s8[7340032]{0:T(1024)(128)(4,1)}), s8[4194304]{0:T(1024)(128)(4,1)S(1)}, s32[]{:S(2)}) async-start(s8[7340032]{0:T(1024)(128)(4,1)} %bitcast.65), calls=%async_computation | async-start | bytes 8388608
  42.5 16.0 %slice-start.2 = ((s8[7340032]{0:T(1024)(128)(4,1)}), s8[4194304]{0:T(1024)(128)(4,1)S(1)}, s32[]{:S(2)}) async-start(s8[7340032]{0:T(1024)(128)(4,1)} %bitcast.67), calls=%async_computation.2 | async-start | bytes 8388608
  43.1 15.3 %slice-start.1 = ((s8[7340032]{0:T(1024)(128)(4,1)}), s8[3145728]{0:T(1024)(128)(4,1)S(1)}, s32[]{:S(2)}) async-start(s8[7340032]{0:T(1024)(128)(4,1)} %bitcast.65), calls=%async_computation.1 | async-start | bytes 6291456
  43.1 15.3 %slice-start.3 = ((s8[7340032]{0:T(1024)(128)(4,1)}), s8[3145728]{0:T(1024)(128)(4,1)S(1)}, s32[]{:S(2)}) async-start(s8[7340032]{0:T(1024)(128)(4,1)} %bitcast.67), calls=%async_computation.3 | async-start | bytes 6291456
  43.1 15.3 %copy-start.3 = (f32[8192]{0:T(1024)S(1)}, f32[8192]{0:T(1024)}, u32[]{:S(2)}) copy-start(f32[8192]{0:T(1024)} %param.19) | copy-start | bytes 98308
  43.1 6.1 %collective-permute-start.14 = (bf16[16,512]{1,0:T(8,128)(2,1)S(1)}, bf16[16,512]{1,0:T(8,128)(2,1)S(1)}, u32[]{:S(2)}, u32[]{:S(2)}) collective-permute-start(bf16[16,512]{1,0:T(8,128)(2,1)S(1)} %shard_map.152.mine_ref), channel_id=1, source_target_pairs={{2,16},{6,20},{10,24},{14,28},{16,2},{20,6},{24,10},{28,14},{3,17}... | collective-permute-start | bytes 49160 | tf_op jit(solution)/shard_map/ppermute | solution.py:536
  43.9 6.7 %collective-permute-start.13 = (bf16[16,512]{1,0:T(8,128)(2,1)S(1)}, bf16[16,512]{1,0:T(8,128)(2,1)S(1)}, u32[]{:S(2)}, u32[]{:S(2)}) collective-permute-start(bf16[16,512]{1,0:T(8,128)(2,1)S(1)} %shard_map.152.mine_ref), channel_id=1, source_target_pairs={{2,0},{0,16},{6,4},{4,20},{10,8},{8,24},{14,12},{12,28},{16,18},{1... | collective-permute-start | bytes 49160 | tf_op jit(solution)/shard_map/ppermute | solution.py:535
  50.7 3.8 %collective-permute-start.15 = (bf16[16,512]{1,0:T(8,128)(2,1)S(1)}, bf16[16,512]{1,0:T(8,128)(2,1)S(1)}, u32[]{:S(2)}, u32[]{:S(2)}) collective-permute-start(bf16[16,512]{1,0:T(8,128)(2,1)S(1)} %shard_map.153.one_ref), channel_id=1, source_target_pairs={{0,8},{4,12},{8,0},{12,4},{16,24},{20,28},{24,16},{28,20},{1,9},{5... | collective-permute-start | bytes 49160 | tf_op jit(solution)/shard_map/ppermute | solution.py:24
  54.5 3.9 %collective-permute-start.16 = (bf16[16,1024]{1,0:T(8,128)(2,1)S(1)}, bf16[16,1024]{1,0:T(8,128)(2,1)S(1)}, u32[]{:S(2)}, u32[]{:S(2)}) collective-permute-start(bf16[16,1024]{1,0:T(8,128)(2,1)S(1)} %shard_map.154.one_ref), channel_id=1, source_target_pairs={{0,4},{4,0},{8,12},{12,8},{16,20},{20,16},{24,28},{28,24},{1,5},{5... | collective-permute-start | bytes 98312 | tf_op jit(solution)/shard_map/ppermute | solution.py:24
  58.4 1.3 %collective-permute-start.17 = (bf16[16,2048]{1,0:T(8,128)(2,1)S(1)}, bf16[16,2048]{1,0:T(8,128)(2,1)S(1)}, u32[]{:S(2)}, u32[]{:S(2)}) collective-permute-start(bf16[16,2048]{1,0:T(8,128)(2,1)S(1)} %shard_map.155.refs_2_), channel_id=1, source_target_pairs={{0,1},{1,0},{2,3},{3,2},{4,5},{5,4},{6,7},{7,6},{8,9},{9,8},{10,11... | collective-permute-start | bytes 196616 | tf_op jit(solution)/shard_map/ppermute | solution.py:24
  60.8 4.6 %collective-permute-start.18 = (bf16[16,1920]{1,0:T(8,128)(2,1)S(1)}, bf16[16,1920]{1,0:T(8,128)(2,1)S(1)}, u32[]{:S(2)}, u32[]{:S(2)}) collective-permute-start(bf16[16,1920]{1,0:T(8,128)(2,1)S(1)} %shard_map.158), channel_id=1, source_target_pairs={{0,2},{2,0},{1,3},{3,1},{4,6},{6,4},{5,7},{7,5},{8,10},{10,8},{9,1... | collective-permute-start | bytes 184328 | tf_op jit(solution)/shard_map/ppermute | solution.py:24
  66.8 1.3 %collective-permute-start.19 = (bf16[8,4096]{1,0:T(8,128)(2,1)S(1)}, bf16[8,4096]{1,0:T(8,128)(2,1)S(1)}, u32[]{:S(2)}, u32[]{:S(2)}) collective-permute-start(bf16[8,4096]{1,0:T(8,128)(2,1)S(1)} %get-tuple-element.60), channel_id=1, source_target_pairs={{0,1},{1,0},{2,3},{3,2},{4,5},{5,4},{6,7},{7,6},{8,9},{9,8},{10,11... | collective-permute-start | bytes 196616 | tf_op jit(solution)/shard_map/ppermute | solution.py:24
  68.1 4.0 %collective-permute-start.20 = (bf16[4,4096]{1,0:T(4,128)(2,1)S(1)}, bf16[4,4096]{1,0:T(4,128)(2,1)S(1)}, u32[]{:S(2)}, u32[]{:S(2)}) collective-permute-start(bf16[4,4096]{1,0:T(4,128)(2,1)S(1)} %select_convert_fusion), channel_id=1, source_target_pairs={{0,4},{4,0},{8,12},{12,8},{16,20},{20,16},{24,28},{28,24},{1,5},{5... | collective-permute-start | bytes 98312 | tf_op jit(solution)/shard_map/ppermute | solution.py:24
  72.3 4.4 %collective-permute-start.21 = (bf16[1,4096]{1,0:T(2,128)(2,1)S(1)}, bf16[1,4096]{1,0:T(2,128)(2,1)S(1)}, u32[]{:S(2)}, u32[]{:S(2)}) collective-permute-start(bf16[1,4096]{1,0:T(2,128)(2,1)S(1)} %get-tuple-element.68), channel_id=1, source_target_pairs={{0,8},{4,12},{8,0},{12,4},{16,24},{20,28},{24,16},{28,20},{1,9},{5... | collective-permute-start | bytes 24584 | tf_op jit(solution)/shard_map/ppermute | solution.py:24
  74.1 5.5 %collective-permute-start.23 = (bf16[1,4096]{1,0:T(2,128)(2,1)S(1)}, bf16[1,4096]{1,0:T(2,128)(2,1)S(1)}, u32[]{:S(2)}, u32[]{:S(2)}) collective-permute-start(bf16[1,4096]{1,0:T(2,128)(2,1)S(1)} %get-tuple-element.69), channel_id=1, source_target_pairs={{0,24},{4,28},{8,16},{12,20},{16,8},{20,12},{24,0},{28,4},{1,25},{... | collective-permute-start | bytes 24584 | tf_op jit(solution)/shard_map/ppermute | solution.py:24
  76.7 4.6 %collective-permute-start.22 = (bf16[1,4096]{1,0:T(2,128)(2,1)S(1)}, bf16[1,4096]{1,0:T(2,128)(2,1)S(1)}, u32[]{:S(2)}, u32[]{:S(2)}) collective-permute-start(bf16[1,4096]{1,0:T(2,128)(2,1)S(1)} %get-tuple-element.70), channel_id=1, source_target_pairs={{0,16},{4,20},{8,24},{12,28},{16,0},{20,4},{24,8},{28,12},{1,17},{... | collective-permute-start | bytes 24584 | tf_op jit(solution)/shard_map/ppermute | solution.py:24
  (6 other events, 24.9 us)
